TPU v7x, 32 devices: a 4x2x2 block of a 4x4x8 slice. The times are simulated.
32 devices in a mesh: stage: 4 (over y, z), data: 8 (over x, core).
Axes of the slice: x: 4, y: 2, z: 2, core: 2. Of those that a mesh axis runs over, the one named last changes fastest.
The devices are a block of a 4x4x8 slice.
Arguments:
- w_master: float32 [32, 768, 3072], P('stage', 'data'), parts along dimension 0
- momentum: float32 [32, 768, 3072], P('stage', 'data'), parts along dimension 0
- grad: bfloat16 [32, 768, 3072], P('stage', 'data'), parts along dimension 0
Outputs:
- output 1: bfloat16 [32, 768, 3072], P('stage'), parts along dimension 0
- output 2: float32 [32, 768, 3072], P('stage', 'data'), parts along dimension 0
There are 4 independent parts. A program takes and returns all parts, laid end to end along the dimension named above; each array names one.
All inputs are finite; a program needn't handle non-finite values.
Results may differ from a plain program's by a relative error of at most 0.00643818.
Values are sent between devices in bfloat16 or wider.
A program may use at most 768 MiB of HBM per device.

v0:
```python
import math
import jax
import jax.numpy as jnp
from jax import lax
from jax.sharding import PartitionSpec as P

NS_ITERS = 5
MOMENTUM = 0.95
LEARN_RATE = 0.02
WEIGHT_DECAY = 0.1
NORM_EPS = 1e-7
COEF_A = 3.4445
COEF_B = -4.7750
COEF_C = 2.0315


def newton_schulz(x_mat):
    wide = x_mat.shape[1] <= x_mat.shape[2]
    for iteration in range(NS_ITERS):
        if wide:
            gram_mat = jnp.einsum("kip,kjp->kij", x_mat, x_mat, preferred_element_type=jnp.float32)
        else:
            gram_mat = jnp.einsum("kpi,kpj->kij", x_mat, x_mat, preferred_element_type=jnp.float32)
        gram_mat = gram_mat.astype(jnp.bfloat16)
        square = jnp.einsum("kij,kjl->kil", gram_mat, gram_mat, preferred_element_type=jnp.float32)
        poly_mat = (COEF_B * gram_mat.astype(jnp.float32) + COEF_C * square).astype(jnp.bfloat16)
        if wide:
            prod_mat = jnp.einsum("kij,kjp->kip", poly_mat, x_mat, preferred_element_type=jnp.float32)
        else:
            prod_mat = jnp.einsum("kpj,kij->kpi", x_mat, poly_mat, preferred_element_type=jnp.float32)
        x_mat = (COEF_A * x_mat.astype(jnp.float32) + prod_mat).astype(jnp.bfloat16)
    return x_mat


def solution(mesh):
    group = mesh.shape["data"]
    row_spec = P("stage", "data", None)
    full_spec = P("stage", None, None)

    def local_step(w_rows, mom_rows, grad_rows):
        mat_count, rows_dev, col_count = mom_rows.shape
        own_count = mat_count // group
        rms_scale = 0.2 * math.sqrt(max(rows_dev * group, col_count))
        mom_new = MOMENTUM * mom_rows + grad_rows.astype(jnp.float32)
        sq_total = lax.psum(jnp.sum(mom_new * mom_new, axis=(1, 2)), "data")
        owned = lax.all_to_all(mom_new.astype(jnp.bfloat16), "data", 0, 1, tiled=True)
        my_index = lax.axis_index("data")
        sq_owned = lax.dynamic_slice_in_dim(sq_total, my_index * own_count, own_count)
        x_mat = (owned.astype(jnp.float32) / (jnp.sqrt(sq_owned)[:, None, None] + NORM_EPS)).astype(jnp.bfloat16)
        x_mat = newton_schulz(x_mat)
        ortho_rows = lax.all_to_all(x_mat, "data", 1, 0, tiled=True)
        w_new = w_rows - LEARN_RATE * (ortho_rows.astype(jnp.float32) * rms_scale + WEIGHT_DECAY * w_rows)
        params = lax.all_gather(w_new.astype(jnp.bfloat16), "data", axis=1, tiled=True)
        return params, mom_new

    return jax.shard_map(local_step, mesh=mesh, in_specs=(row_spec, row_spec, row_spec), out_specs=(full_spec, row_spec), check_vma=False)
```

profile of v0, /device:TPU:81, one launch (start us, length us, event | category | flops | bytes accessed | tf_op | source)
XLA Modules:
  0.0 533.2 jit_solution(15772970677322932360)
XLA Ops:
  7.2 6.9 %multiply_reduce_fusion = (f32[8]{0:T(128)S(1)}, f32[8,96,3072]{2,1,0:T(8,128)S(1)}) fusion(bf16[8,96,3072]{2,1,0:T(8,128)(2,1)} %param.5, f32[8,96,3072]{2,1,0:T(8,128)} %param.4), kind=kLoop, calls=%fused_computation.8 | loop fusion | flops 11796472 | bytes 23592992 | tf_op jit(solution)/shard_map/reduce_sum | solution.py:45
  14.1 0.0 copy-start
  14.1 3.7 copy-done
  17.8 2.9 convert_element_type.145
  20.7 6.5 %all-to-all-start = ((bf16[8,96,3072]{2,1,0:T(8,128)(2,1)}), bf16[8,96,3072]{2,1,0:T(8,128)(2,1)}, u32[]{:S(2)}, u32[]{:S(2)}) async-start(bf16[8,96,3072]{2,1,0:T(8,128)(2,1)} %convert_element_type.145), calls=%async_computation | async-start | bytes 9437184 | tf_op jit(solution)/shard_map/all_to_all | solution.py:46
  27.2 0.0 all-gather.2.cloned.1.call-start
  27.2 58.7 %psum.7 = f32[8]{0:T(128)S(1)} all-reduce(f32[8]{0:T(128)S(1)} %get-tuple-element.2), channel_id=1, replica_groups=mesh['stage'=4,'data'=8] {'data'}, use_global_device_ids=true, to_apply=%region_1.0 | all-reduce | flops 8 | bytes 64 | tf_op jit(solution)/shard_map/psum | solution.py:45
  86.0 0.6 dynamic_slice.3
  87.1 0.0 all-to-all-done
  87.1 3.4 divide_convert_fusion
  90.6 0.0 copy-start.1
  90.6 2.2 copy-done.1
  92.7 3.9 convolution_convert_fusion.4
  96.6 10.1 %add_convert_fusion.4 = bf16[768,3072]{1,0:T(8,128)(2,1)} fusion(bf16[768,3072]{1,0:T(8,128)(2,1)} %bitcast.38, bf16[768,768]{1,0:T(8,128)(2,1)S(1)} %convolution_convert_fusion.4), kind=kOutput, calls=%fused_computation.6 | convolution fusion | flops 4542234624 | bytes 10616832 | tf_op jit(solution)/shard_map/kij,kjp->kip/dot_general | solution.py:28
  106.7 7.6 %convolution_convert_fusion.3 = bf16[768,768]{1,0:T(8,128)(2,1)S(1)} fusion(bf16[768,3072]{1,0:T(8,128)(2,1)} %add_convert_fusion.4), kind=kOutput, calls=%fused_computation.19 | convolution fusion | flops 3624468480 | bytes 5898240 | tf_op jit(solution)/shard_map/kip,kjp->kij/dot_general | solution.py:21
  114.3 10.5 %add_convert_fusion.3 = bf16[768,3072]{1,0:T(8,128)(2,1)} fusion(bf16[768,3072]{1,0:T(8,128)(2,1)} %add_convert_fusion.4, bf16[768,768]{1,0:T(8,128)(2,1)S(1)} %convolution_convert_fusion.3), kind=kOutput, calls=%fused_computation.5 | convolution fusion | flops 4542234624 | bytes 10616832 | tf_op jit(solution)/shard_map/kij,kjp->kip/dot_general | solution.py:28
  124.8 7.7 %convolution_convert_fusion.2 = bf16[768,768]{1,0:T(8,128)(2,1)S(1)} fusion(bf16[768,3072]{1,0:T(8,128)(2,1)} %add_convert_fusion.3), kind=kOutput, calls=%fused_computation.18 | convolution fusion | flops 3624468480 | bytes 5898240 | tf_op jit(solution)/shard_map/kip,kjp->kij/dot_general | solution.py:21
  132.5 10.1 %add_convert_fusion.2 = bf16[768,3072]{1,0:T(8,128)(2,1)} fusion(bf16[768,3072]{1,0:T(8,128)(2,1)} %add_convert_fusion.3, bf16[768,768]{1,0:T(8,128)(2,1)S(1)} %convolution_convert_fusion.2), kind=kOutput, calls=%fused_computation.4 | convolution fusion | flops 4542234624 | bytes 10616832 | tf_op jit(solution)/shard_map/kij,kjp->kip/dot_general | solution.py:28
  142.6 7.6 %convolution_convert_fusion.1 = bf16[768,768]{1,0:T(8,128)(2,1)S(1)} fusion(bf16[768,3072]{1,0:T(8,128)(2,1)} %add_convert_fusion.2), kind=kOutput, calls=%fused_computation.17 | convolution fusion | flops 3624468480 | bytes 5898240 | tf_op jit(solution)/shard_map/kip,kjp->kij/dot_general | solution.py:21
  150.2 10.1 %add_convert_fusion.1 = bf16[768,3072]{1,0:T(8,128)(2,1)} fusion(bf16[768,3072]{1,0:T(8,128)(2,1)} %add_convert_fusion.2, bf16[768,768]{1,0:T(8,128)(2,1)S(1)} %convolution_convert_fusion.1), kind=kOutput, calls=%fused_computation.3 | convolution fusion | flops 4542234624 | bytes 10616832 | tf_op jit(solution)/shard_map/kij,kjp->kip/dot_general | solution.py:28
  160.4 7.7 %convolution_convert_fusion = bf16[768,768]{1,0:T(8,128)(2,1)S(1)} fusion(bf16[768,3072]{1,0:T(8,128)(2,1)} %add_convert_fusion.1), kind=kOutput, calls=%fused_computation.16 | convolution fusion | flops 3624468480 | bytes 5898240 | tf_op jit(solution)/shard_map/kip,kjp->kij/dot_general | solution.py:21
  168.1 10.1 %fusion = bf16[1,768,3072]{2,1,0:T(8,128)(2,1)} fusion(bf16[768,3072]{1,0:T(8,128)(2,1)} %add_convert_fusion.1, bf16[768,768]{1,0:T(8,128)(2,1)S(1)} %convolution_convert_fusion), kind=kOutput, calls=%fused_computation.10 | convolution fusion | flops 4542234624 | bytes 10616832 | tf_op jit(solution)/shard_map/kij,kjp->kip/dot_general | solution.py:28
  178.2 9.5 %copy.8 = bf16[1,768,3072]{2,0,1:T(2,128)(2,1)} copy(bf16[1,768,3072]{2,1,0:T(8,128)(2,1)} %fusion) | data formatting | bytes 9437184 | tf_op jit(solution)/shard_map/convert_element_type | solution.py:31
  187.7 0.5 broadcast.78
  188.2 28.8 %reduce = bf16[768,3072]{1,0:T(8,128)(2,1)} reduce(bf16[768,1,3072]{2,1,0:T(2,128)(2,1)} %bitcast.35, bf16[]{:T(256)} %broadcast.78), dimensions={1}, to_apply=%bitcast.34.reduce_sub_computation | reduce | bytes 9437186
  217.0 8.2 %reshape.161 = bf16[8,2,147456]{2,1,0:T(2,128)(2,1)} reshape(bf16[768,3072]{1,0:T(8,128)(2,1)} %reduce) | data formatting | bytes 9437184
  225.2 60.4 %all_to_all.8 = bf16[8,2,147456]{2,1,0:T(2,128)(2,1)} all-to-all(bf16[8,2,147456]{2,1,0:T(2,128)(2,1)} %reshape.161), channel_id=1, replica_groups=mesh['stage'=4,'data'=8] {'data'}, dimensions={0} | all-to-all | bytes 9437184 | tf_op jit(solution)/shard_map/all_to_all | solution.py:51
  285.6 9.2 %reshape.162 = bf16[768,1,3072]{2,1,0:T(2,128)(2,1)} reshape(bf16[8,2,147456]{2,1,0:T(2,128)(2,1)} %all_to_all.8) | data formatting | bytes 9437184
  294.8 14.4 %convert_multiply_fusion = f32[1,768,3072]{2,0,1:T(1,128)S(1)} fusion(bf16[768,1,3072]{2,1,0:T(2,128)(2,1)} %reshape.162), kind=kLoop, calls=%fused_computation.1 | loop fusion | flops 4718592 | bytes 14155776 | tf_op jit(solution)/shard_map/mul | solution.py:52
  309.2 5.9 %copy.6 = f32[1,768,3072]{2,1,0:T(8,128)} copy(f32[1,768,3072]{2,0,1:T(1,128)S(1)} %convert_multiply_fusion) | data formatting | bytes 18874368
  315.1 11.0 %subtract_convert_fusion = bf16[8,96,3072]{2,1,0:T(8,128)(2,1)} fusion(f32[8,96,3072]{2,1,0:T(8,128)} %param.3, f32[8,96,3072]{2,1,0:T(8,128)} %bitcast.36), kind=kLoop, calls=%fused_computation | loop fusion | flops 11796480 | bytes 23592960 | tf_op jit(solution)/shard_map/convert_element_type | solution.py:53
  326.1 0.1 all-gather.2.cloned.1.call-update
  326.2 174.6 %all-gather.2.cloned.1.call-done = bf16[8,768,3072]{2,1,0:T(8,128)(2,1)} async-done(((bf16[8,96,3072]{2,1,0:T(8,128)(2,1)}), bf16[8,768,3072]{2,1,0:T(8,128)(2,1)}) %all-gather.2.cloned.1.call-update) | async-done | bytes 37748752 | tf_op jit(solution)/shard_map/all_gather | solution.py:53
  500.8 25.4 %copy.10 = bf16[8,768,3072]{2,1,0:T(8,128)(2,1)} copy(bf16[8,768,3072]{2,1,0:T(8,128)(2,1)} %all-gather.2.cloned.1.call-done) | data formatting | bytes 75497472
Async XLA Ops:
  14.1 3.7 copy-start
  20.7 66.4 %all-to-all-start = ((bf16[8,96,3072]{2,1,0:T(8,128)(2,1)}), bf16[8,96,3072]{2,1,0:T(8,128)(2,1)}, u32[]{:S(2)}, u32[]{:S(2)}) async-start(bf16[8,96,3072]{2,1,0:T(8,128)(2,1)} %convert_element_type.145), calls=%async_computation | async-start | bytes 9437184 | tf_op jit(solution)/shard_map/all_to_all | solution.py:46
  27.2 473.5 %all-gather.2.cloned.1.call-start = ((), (), s32[]{:S(2)}) async-start(), calls=%async_computation.2 | async-start | bytes 42467328 | tf_op jit(solution)/shard_map/all_gather | solution.py:53
  90.6 2.2 copy-start.1
Sparse Core Ops, SparseCore 0:
  326.3 174.4 all-gather.1
where the time goes:
time: 537 us; the launch traced here: 533 us
  waiting for transfers between devices  175 us (33%)
  blocking collectives  119 us (22%)
  matrix products  85.4 us (16%)
  other arithmetic  67.5 us (13%)
  local copies, waits for them, and re-layouts  65.2 us (12%)
  between operations  15 us (3%)
  starting transfers between devices  6.51 us (1%)
    all_gather x1, waiting for transfers between devices, local_step(): lax.all_gather(w_new.astype(jnp.bfloat16), 'data', axis=1, tiled=True)  175 us
    all_to_all x1, blocking collectives, local_step(): ortho_rows = lax.all_to_all(x_mat, 'data', 1, 0, tiled=True)  60.4 us
    psum x1, blocking collectives, local_step(): sq_total = lax.psum(jnp.sum(mom_new * mom_new, axis=(1, 2)), 'data')  58.7 us
    unnamed x9, local copies, waits for them, and re-layouts  55.1 us
    dot_general x5, matrix products, newton_schulz(): jnp.einsum('kij,kjp->kip', poly_mat, x_mat, preferred_element_type=jnp.fl...  50.9 us
    dot_general x5, matrix products, newton_schulz(): jnp.einsum('kip,kjp->kij', x_mat, x_mat, preferred_element_type=jnp.float32)  34.5 us
    unnamed x1, other arithmetic  28.8 us
    mul x1, other arithmetic, local_step(): ortho_rows.astype(jnp.float32) * rms_scale + WEIGHT_DECAY * w_rows  14.4 us
  transfers between devices with their start and end apart: 2, of which 1 were waited for; matrix products, arithmetic and copies ran while one was open for 0% of the time, Pallas kernels for 0%

commit v1 on v0

v1 whole, which is shorter than its diff:
```python
import functools
import math

import jax
import jax.numpy as jnp
from jax import lax
from jax.experimental import pallas as pl
from jax.experimental.pallas import tpu as pltpu
from jax.sharding import PartitionSpec as P

NS_ITERS = 5
MOMENTUM = 0.95
LEARN_RATE = 0.02
WEIGHT_DECAY = 0.1
NORM_EPS = 1e-7
COEF_A = 3.4445
COEF_B = -4.7750
COEF_C = 2.0315

MESH = pl.DeviceIdType.MESH
TILE = 256


def momentum_kernel(mom_ref, grad_ref, new_ref, low_ref, sq_ref):
    mom_new = MOMENTUM * mom_ref[0] + grad_ref[0].astype(jnp.float32)
    new_ref[0] = mom_new
    low_ref[0] = mom_new.astype(jnp.bfloat16)
    square = mom_new * mom_new
    rows, cols = square.shape
    lanes = square[:, :128]
    for start in range(128, cols, 128):
        lanes = lanes + square[:, start : start + 128]
    tile = lanes[:8]
    for start in range(8, rows, 8):
        tile = tile + lanes[start : start + 8]
    sq_ref[0] = tile


def momentum_step(mom, grad):
    mats, rows, cols = mom.shape
    block = pl.BlockSpec((1, rows, cols), lambda i: (i, 0, 0))
    return pl.pallas_call(
        momentum_kernel,
        grid=(mats,),
        in_specs=[block, block],
        out_specs=[block, block, pl.BlockSpec((1, 8, 128), lambda i: (i, 0, 0))],
        out_shape=[
            jax.ShapeDtypeStruct(mom.shape, jnp.float32),
            jax.ShapeDtypeStruct(mom.shape, jnp.bfloat16),
            jax.ShapeDtypeStruct((mats, 8, 128), jnp.float32),
        ],
    )(mom, grad)


def muon_kernel(group, low, sq_in, w, out, x, gram, poly, rows2, relay_a, relay_c, w2, back, new, sq, send, recv, go):
    chips = group // 2
    mats, rows, cols = low.shape
    pair = 2 * rows
    dim = pair * chips
    rms_scale = 0.2 * math.sqrt(max(dim, cols))
    me = lax.axis_index("data")
    c, k = lax.div(me, 2), lax.rem(me, 2)
    sib = 2 * c + 1 - k
    right, left, opp = (lax.rem(c + step, chips) for step in (1, chips - 1, 2))

    def peer_of(chip):
        return 2 * chip + k

    sent, slots = [], {}

    def slot(key):
        return slots.setdefault(key, len(slots))

    def push(src, dst, peer, key):
        copy = pltpu.make_async_remote_copy(
            src_ref=src, dst_ref=dst, send_sem=send.at[len(sent)], recv_sem=recv.at[slot(key)],
            device_id={"data": peer}, device_id_type=MESH)
        copy.start()
        sent.append(copy)

    def local(src, dst, key):
        copy = pltpu.make_async_copy(src, dst, recv.at[slot(key)])
        copy.start()

    def arrived(dst, key):
        pltpu.make_async_copy(dst, dst, recv.at[slot(key)]).wait()

    def span(start, size):
        return pl.ds(pl.multiple_of(start, rows), size)

    def own_rows(chip, half=None):
        if half is None:
            return span(chip * pair, pair)
        return span(chip * pair + half * rows, rows)

    barrier = pltpu.get_barrier_semaphore()
    for step in range(1, group):
        pl.semaphore_signal(barrier, inc=1, device_id={"data": lax.rem(me + step, group)}, device_id_type=MESH)
    pl.semaphore_wait(barrier, group - 1)

    for step, chip in enumerate((opp, right, left, c)):
        push(low.at[2 * chip + 1 - k], rows2.at[chip, span(k * rows, rows)], sib, ("swap", step))
        local(low.at[2 * chip + k], rows2.at[chip, span(k * rows, rows)], ("keep", step))
    for step in range(1, group):
        dest = lax.rem(me + step, group)
        push(sq_in.at[dest], sq.at[step], dest, ("sq", step))
    for step, chip in enumerate((c, left, right, opp)):
        push(w.at[2 * chip + 1 - k], w2.at[chip, span(k * rows, rows)], sib, ("wswap", step))
        local(w.at[2 * chip + k], w2.at[chip, span(k * rows, rows)], ("wkeep", step))

    @pl.when(k == 1)
    def _():
        pl.semaphore_wait(go, 1)

    def swapped(step, chip):
        arrived(rows2.at[chip, span((1 - k) * rows, rows)], ("swap", step))
        arrived(rows2.at[chip, span(k * rows, rows)], ("keep", step))

    swapped(0, opp)
    push(rows2.at[opp, pl.ds(0, rows)], relay_a.at[0], peer_of(right), "a_relay_l")
    push(rows2.at[opp, pl.ds(rows, rows)], relay_a.at[1], peer_of(left), "a_relay_r")
    swapped(1, right)
    push(rows2.at[right], x.at[own_rows(c)], peer_of(right), "a_left")
    swapped(2, left)
    push(rows2.at[left], x.at[own_rows(c)], peer_of(left), "a_right")
    arrived(relay_a.at[0], "a_relay_l")
    push(relay_a.at[0], x.at[own_rows(left, 0)], peer_of(right), "a_opp_l")
    arrived(relay_a.at[1], "a_relay_r")
    push(relay_a.at[1], x.at[own_rows(right, 1)], peer_of(left), "a_opp_r")
    swapped(3, c)

    total = sq_in[me]
    for step in range(1, group):
        arrived(sq.at[step], ("sq", step))
        total = total + sq[step]
    norm = jnp.sqrt(jnp.sum(total, keepdims=True))
    inverse = 1.0 / (norm + NORM_EPS)

    chunk = 32

    def scale(get, base, size):
        @pl.loop(0, size // chunk)
        def _(r):
            part = pl.ds(pl.multiple_of(base + r * chunk, chunk), chunk)
            x[part, :] = (get(r).astype(jnp.float32) * inverse).astype(jnp.bfloat16)

    def in_place(base):
        return lambda r: x[pl.ds(pl.multiple_of(base + r * chunk, chunk), chunk), :]

    scale(lambda r: rows2[c, pl.ds(pl.multiple_of(r * chunk, chunk), chunk), :], c * pair, pair)
    arrived(x.at[own_rows(left)], "a_left")
    scale(in_place(left * pair), left * pair, pair)
    arrived(x.at[own_rows(right)], "a_right")
    scale(in_place(right * pair), right * pair, pair)
    arrived(x.at[own_rows(opp, 0)], "a_opp_l")
    arrived(x.at[own_rows(opp, 1)], "a_opp_r")

    @pl.when(k == 0)
    def _():
        pl.semaphore_signal(go, inc=1, device_id={"data": sib}, device_id_type=MESH)

    scale(in_place(opp * pair), opp * pair, pair)

    @pl.loop(0, NS_ITERS)
    def _(_):
        @pl.loop(0, dim // TILE)
        def _(j):
            part = pl.ds(pl.multiple_of(j * TILE, TILE), TILE)
            gram[:, part] = lax.dot_general(
                x[...], x[part, :], (((1,), (1,)), ((), ())), preferred_element_type=jnp.float32
            ).astype(jnp.bfloat16)

        @pl.loop(0, dim // TILE)
        def _(j):
            part = pl.ds(pl.multiple_of(j * TILE, TILE), TILE)
            square = jnp.dot(gram[...], gram[:, part], preferred_element_type=jnp.float32)
            poly[:, part] = (COEF_B * gram[:, part].astype(jnp.float32) + COEF_C * square).astype(jnp.bfloat16)

        @pl.loop(0, cols // (2 * TILE))
        def _(j):
            part = pl.ds(pl.multiple_of(j * 2 * TILE, 2 * TILE), 2 * TILE)
            old = x[:, part]
            prod = jnp.dot(poly[...], old, preferred_element_type=jnp.float32)
            x[:, part] = (COEF_A * old.astype(jnp.float32) + prod).astype(jnp.bfloat16)

    push(x.at[own_rows(opp, 0)], relay_c.at[0], peer_of(right), "c_relay_l")
    push(x.at[own_rows(opp, 1)], relay_c.at[1], peer_of(left), "c_relay_r")
    push(x.at[own_rows(right)], back.at[c], peer_of(right), "c_left")
    push(x.at[own_rows(left)], back.at[c], peer_of(left), "c_right")

    step_rows = 16
    order = (0, chips - 1, 1, 2)

    def update(step, get):
        chip = lax.rem(c + order[step], chips)

        @pl.loop(0, pair // step_rows)
        def _(r):
            part = pl.ds(pl.multiple_of(r * step_rows, step_rows), step_rows)
            w_part = w2[chip, part, :]
            ortho = get(chip, r).astype(jnp.float32) * rms_scale
            new[chip, part, :] = (w_part - LEARN_RATE * (ortho + WEIGHT_DECAY * w_part)).astype(jnp.bfloat16)

        place = out.at[2 * chip + k, own_rows(c)]
        push(new.at[chip], place, peer_of(right), ("g_left", step))
        push(new.at[chip], place, peer_of(left), ("g_right", step))
        push(new.at[chip], place, sib, ("s_own", step))
        local(new.at[chip], place, ("own", step))

    for step, chip in enumerate((c, left, right, opp)):
        arrived(w2.at[chip, span((1 - k) * rows, rows)], ("wswap", step))
        arrived(w2.at[chip, span(k * rows, rows)], ("wkeep", step))
    update(0, lambda chip, r: x[pl.ds(pl.multiple_of(c * pair + r * step_rows, step_rows), step_rows), :])
    arrived(relay_c.at[0], "c_relay_l")
    push(relay_c.at[0], back.at[left, pl.ds(0, rows)], peer_of(right), "c_opp_l")
    arrived(relay_c.at[1], "c_relay_r")
    push(relay_c.at[1], back.at[right, pl.ds(rows, rows)], peer_of(left), "c_opp_r")

    def from_back(chip, r):
        return back[chip, pl.ds(pl.multiple_of(r * step_rows, step_rows), step_rows), :]

    arrived(back.at[left], "c_left")
    update(1, from_back)
    arrived(back.at[right], "c_right")
    update(2, from_back)
    arrived(back.at[opp, pl.ds(0, rows)], "c_opp_l")
    arrived(back.at[opp, pl.ds(rows, rows)], "c_opp_r")
    update(3, from_back)

    for step in range(chips):
        mat_l = 2 * lax.rem(left + order[step], chips) + k
        mat_r = 2 * lax.rem(right + order[step], chips) + k
        whole_l, whole_r = out.at[mat_l, own_rows(left)], out.at[mat_r, own_rows(right)]
        part_l, part_r = out.at[mat_l, own_rows(left, 0)], out.at[mat_r, own_rows(right, 1)]
        arrived(whole_l, ("g_left", step))
        push(part_l, part_l, peer_of(right), ("f_left", step))
        push(whole_l, whole_l, sib, ("s_left", step))
        arrived(whole_r, ("g_right", step))
        push(part_r, part_r, peer_of(left), ("f_right", step))
        push(whole_r, whole_r, sib, ("s_right", step))
    for step in range(chips):
        mat_o = 2 * lax.rem(opp + order[step], chips) + k
        part_l, part_r = out.at[mat_o, own_rows(opp, 0)], out.at[mat_o, own_rows(opp, 1)]
        arrived(part_l, ("f_left", step))
        push(part_l, part_l, sib, ("s_far_l", step))
        arrived(part_r, ("f_right", step))
        push(part_r, part_r, sib, ("s_far_r", step))
    for step in range(chips):
        mat = 2 * lax.rem(c + order[step], chips)
        arrived(out.at[mat + k, own_rows(c)], ("own", step))
        arrived(out.at[mat + 1 - k, own_rows(c)], ("s_own", step))
        arrived(out.at[2 * lax.rem(left + order[step], chips) + 1 - k, own_rows(left)], ("s_left", step))
        arrived(out.at[2 * lax.rem(right + order[step], chips) + 1 - k, own_rows(right)], ("s_right", step))
        mat_o = 2 * lax.rem(opp + order[step], chips) + 1 - k
        arrived(out.at[mat_o, own_rows(opp, 0)], ("s_far_l", step))
        arrived(out.at[mat_o, own_rows(opp, 1)], ("s_far_r", step))
    for copy in sent:
        copy.wait_send()


def muon_step(group, low, sq_in, w):
    mats, rows, cols = low.shape
    chips, pair = group // 2, 2 * rows
    dim = pair * chips
    hbm = pl.BlockSpec(memory_space=pl.ANY)
    return pl.pallas_call(
        functools.partial(muon_kernel, group),
        in_specs=[hbm, pl.BlockSpec(memory_space=pltpu.VMEM), hbm],
        out_specs=hbm,
        out_shape=jax.ShapeDtypeStruct((mats, dim, cols), jnp.bfloat16),
        scratch_shapes=[
            pltpu.VMEM((dim, cols), jnp.bfloat16),
            pltpu.VMEM((dim, dim), jnp.bfloat16),
            pltpu.VMEM((dim, dim), jnp.bfloat16),
            pltpu.VMEM((chips, pair, cols), jnp.bfloat16),
            pltpu.VMEM((2, rows, cols), jnp.bfloat16),
            pltpu.VMEM((2, rows, cols), jnp.bfloat16),
            pltpu.VMEM((chips, pair, cols), jnp.float32),
            pltpu.VMEM((chips, pair, cols), jnp.bfloat16),
            pltpu.VMEM((chips, pair, cols), jnp.bfloat16),
            pltpu.VMEM((group, 8, 128), jnp.float32),
            pltpu.SemaphoreType.DMA((80,)),
            pltpu.SemaphoreType.DMA((80,)),
            pltpu.SemaphoreType.REGULAR,
        ],
        compiler_params=pltpu.CompilerParams(
            collective_id=0, has_side_effects=True, vmem_limit_bytes=58 * 1024 * 1024
        ),
    )(low, sq_in, w)


def solution(mesh):
    group = mesh.shape["data"]
    row_spec = P("stage", "data", None)
    full_spec = P("stage", None, None)

    def local_step(w_rows, mom_rows, grad_rows):
        mom_new, low, square = momentum_step(mom_rows, grad_rows)
        params = muon_step(group, low, square, w_rows)
        return params, mom_new

    return jax.shard_map(
        local_step, mesh=mesh, in_specs=(row_spec, row_spec, row_spec), out_specs=(full_spec, row_spec), check_vma=False
    )
```

time: 537 us -> 335 us (0.62)
  Pallas kernels: 0 us -> 309 us
  waiting for transfers between devices: 175 us -> 0 us
  blocking collectives: 119 us -> 0 us
  matrix products: 85.4 us -> 0 us
  other arithmetic: 67.5 us -> 0 us
  local copies, waits for them, and re-layouts: 65.2 us -> 25.4 us
  between operations: 15 us -> 0.64 us
  starting transfers between devices: 6.51 us -> 0 us
    pallas_call x0 -> x2, Pallas kernels: none -> 309 us  [the longest x1 296 us: muon_step(): pl.pallas_call(functools.partial(muon_kernel, group), in_specs=[hbm, pl.B...]
    all_gather x1 -> x0, waiting for transfers between devices: 175 us -> none  [local_step(): lax.all_gather(w_new.astype(jnp.bfloat16), 'data', axis=1, tiled=True)]
    dot_general x10 -> x0, matrix products: 85.4 us -> none  [the longest x5 50.9 us: newton_schulz(): jnp.einsum('kij,kjp->kip', poly_mat, x_mat, preferred_element_type=jnp.fl...]
    all_to_all x1 -> x0, blocking collectives: 60.4 us -> none  [local_step(): ortho_rows = lax.all_to_all(x_mat, 'data', 1, 0, tiled=True)]
    psum x1 -> x0, blocking collectives: 58.7 us -> none  [local_step(): sq_total = lax.psum(jnp.sum(mom_new * mom_new, axis=(1, 2)), 'data')]
    unnamed x9 -> x1, local copies, waits for them, and re-layouts: 55.1 us -> 25.4 us
    unnamed x1 -> x0, other arithmetic: 28.8 us -> none
    convert_element_type x3 -> x0, other arithmetic: 17.3 us -> none  [the longest x1 11 us: local_step(): w_new.astype(jnp.bfloat16)]
  transfers between devices with their start and end apart: 2 -> 0, of which waited for: 1 -> 0; matrix products, arithmetic and copies ran while one was open for 0% -> 0% of each run, Pallas kernels for 0% -> 0%
where the time goes in v1:
time: 335 us
  Pallas kernels  309 us (92%)
  local copies, waits for them, and re-layouts  25.4 us (8%)
    pallas_call x1, Pallas kernels, muon_step(): pl.pallas_call(functools.partial(muon_kernel, group), in_specs=[hbm, pl.B...  296 us
    unnamed x1, local copies, waits for them, and re-layouts  25.4 us
    pallas_call x1, Pallas kernels, momentum_step(): pl.pallas_call(momentum_kernel, grid=(mats,), in_specs=[block, block], ou...  12.6 us

profile of v1, /device:TPU:81, one launch (start us, length us, event | category | flops | bytes accessed | tf_op | source)
XLA Modules:
  0.0 334.9 jit_solution(15235234291562986839)
XLA Ops:
  0.6 12.6 %shard_map.50 = (f32[8,96,3072]{2,1,0:T(8,128)}, bf16[8,96,3072]{2,1,0:T(8,128)(2,1)}, f32[8,8,128]{2,1,0:T(8,128)}) custom-call(f32[8,96,3072]{2,1,0:T(8,128)} %mom_ref.1, bf16[8,96,3072]{2,1,0:T(8,128)(2,1)} %grad_ref.1), custom_call_target="tpu_custom_call" | custom-call | tf_op jit(solution)/shard_map/pallas_call | solution.py:42
  13.2 296.3 %shard_map.51 = bf16[8,768,3072]{2,1,0:T(8,128)(2,1)} custom-call(bf16[8,96,3072]{2,1,0:T(8,128)(2,1)} %get-tuple-element.5.low, f32[8,8,128]{2,1,0:T(8,128)} %get-tuple-element.6.sq_in, f32[8,96,3072]{2,1,0:T(8,128)} %w.1), custom_call_target="tpu_custom_call" | custom-call | tf_op jit(solution)/shard_map/pallas_call | solution.py:266
  309.5 25.4 %copy.6 = bf16[8,768,3072]{2,1,0:T(8,128)(2,1)} copy(bf16[8,768,3072]{2,1,0:T(8,128)(2,1)} %shard_map.51) | data formatting | bytes 75497472

commit v2 on v1

--- a/solution.py
+++ b/solution.py
@@ -52,7 +52,7 @@
     )(mom, grad)
 
 
-def muon_kernel(group, low, sq_in, w, out, x, gram, poly, rows2, relay_a, relay_c, w2, back, new, sq, send, recv, go):
+def muon_kernel(group, low, sq_in, w, out, x, gram, poly, relay_a, relay_c, w2, sq, send, recv, go, free):
     chips = group // 2
     mats, rows, cols = low.shape
     pair = 2 * rows
@@ -66,6 +66,9 @@
     def peer_of(chip):
         return 2 * chip + k
 
+    def mine(chip, start=0, size=pair):
+        return out.at[2 * chip + k, pl.ds(pl.multiple_of(c * pair + start, rows), size)]
+
     sent, slots = [], {}
 
     def slot(key):
@@ -77,6 +80,7 @@
             device_id={"data": peer}, device_id_type=MESH)
         copy.start()
         sent.append(copy)
+        return copy
 
     def local(src, dst, key):
         copy = pltpu.make_async_copy(src, dst, recv.at[slot(key)])
@@ -99,8 +103,8 @@
     pl.semaphore_wait(barrier, group - 1)
 
     for step, chip in enumerate((opp, right, left, c)):
-        push(low.at[2 * chip + 1 - k], rows2.at[chip, span(k * rows, rows)], sib, ("swap", step))
-        local(low.at[2 * chip + k], rows2.at[chip, span(k * rows, rows)], ("keep", step))
+        push(low.at[2 * chip + 1 - k], out.at[2 * chip + 1 - k, own_rows(c, k)], sib, ("swap", step))
+        local(low.at[2 * chip + k], mine(chip, k * rows, rows), ("keep", step))
     for step in range(1, group):
         dest = lax.rem(me + step, group)
         push(sq_in.at[dest], sq.at[step], dest, ("sq", step))
@@ -113,16 +117,18 @@
         pl.semaphore_wait(go, 1)
 
     def swapped(step, chip):
-        arrived(rows2.at[chip, span((1 - k) * rows, rows)], ("swap", step))
-        arrived(rows2.at[chip, span(k * rows, rows)], ("keep", step))
+        arrived(mine(chip, (1 - k) * rows, rows), ("swap", step))
+        arrived(mine(chip, k * rows, rows), ("keep", step))
 
     swapped(0, opp)
-    push(rows2.at[opp, pl.ds(0, rows)], relay_a.at[0], peer_of(right), "a_relay_l")
-    push(rows2.at[opp, pl.ds(rows, rows)], relay_a.at[1], peer_of(left), "a_relay_r")
+    mine_sent = [
+        push(mine(opp, 0, rows), relay_a.at[0], peer_of(right), "a_relay_l"),
+        push(mine(opp, rows, rows), relay_a.at[1], peer_of(left), "a_relay_r"),
+    ]
     swapped(1, right)
-    push(rows2.at[right], x.at[own_rows(c)], peer_of(right), "a_left")
+    mine_sent.append(push(mine(right), x.at[own_rows(c)], peer_of(right), "a_left"))
     swapped(2, left)
-    push(rows2.at[left], x.at[own_rows(c)], peer_of(left), "a_right")
+    mine_sent.append(push(mine(left), x.at[own_rows(c)], peer_of(left), "a_right"))
     arrived(relay_a.at[0], "a_relay_l")
     push(relay_a.at[0], x.at[own_rows(left, 0)], peer_of(right), "a_opp_l")
     arrived(relay_a.at[1], "a_relay_r")
@@ -147,7 +153,7 @@
     def in_place(base):
         return lambda r: x[pl.ds(pl.multiple_of(base + r * chunk, chunk), chunk), :]
 
-    scale(lambda r: rows2[c, pl.ds(pl.multiple_of(r * chunk, chunk), chunk), :], c * pair, pair)
+    scale(lambda r: out[2 * c + k, pl.ds(pl.multiple_of(c * pair + r * chunk, chunk), chunk), :], c * pair, pair)
     arrived(x.at[own_rows(left)], "a_left")
     scale(in_place(left * pair), left * pair, pair)
     arrived(x.at[own_rows(right)], "a_right")
@@ -160,6 +166,11 @@
         pl.semaphore_signal(go, inc=1, device_id={"data": sib}, device_id_type=MESH)
 
     scale(in_place(opp * pair), opp * pair, pair)
+
+    for copy in mine_sent:
+        copy.wait_send()
+    for chip in (right, left):
+        pl.semaphore_signal(free, inc=1, device_id={"data": peer_of(chip)}, device_id_type=MESH)
 
     @pl.loop(0, NS_ITERS)
     def _(_):
@@ -183,10 +194,11 @@
             prod = jnp.dot(poly[...], old, preferred_element_type=jnp.float32)
             x[:, part] = (COEF_A * old.astype(jnp.float32) + prod).astype(jnp.bfloat16)
 
+    pl.semaphore_wait(free, 2)
     push(x.at[own_rows(opp, 0)], relay_c.at[0], peer_of(right), "c_relay_l")
     push(x.at[own_rows(opp, 1)], relay_c.at[1], peer_of(left), "c_relay_r")
-    push(x.at[own_rows(right)], back.at[c], peer_of(right), "c_left")
-    push(x.at[own_rows(left)], back.at[c], peer_of(left), "c_right")
+    push(x.at[own_rows(right)], out.at[2 * c + k, own_rows(right)], peer_of(right), "c_left")
+    push(x.at[own_rows(left)], out.at[2 * c + k, own_rows(left)], peer_of(left), "c_right")
 
     step_rows = 16
     order = (0, chips - 1, 1, 2)
@@ -199,32 +211,31 @@
             part = pl.ds(pl.multiple_of(r * step_rows, step_rows), step_rows)
             w_part = w2[chip, part, :]
             ortho = get(chip, r).astype(jnp.float32) * rms_scale
-            new[chip, part, :] = (w_part - LEARN_RATE * (ortho + WEIGHT_DECAY * w_part)).astype(jnp.bfloat16)
-
-        place = out.at[2 * chip + k, own_rows(c)]
-        push(new.at[chip], place, peer_of(right), ("g_left", step))
-        push(new.at[chip], place, peer_of(left), ("g_right", step))
-        push(new.at[chip], place, sib, ("s_own", step))
-        local(new.at[chip], place, ("own", step))
+            out[2 * chip + k, pl.ds(pl.multiple_of(c * pair + r * step_rows, step_rows), step_rows), :] = (w_part - LEARN_RATE * (ortho + WEIGHT_DECAY * w_part)).astype(jnp.bfloat16)
+
+        place = mine(chip)
+        push(place, place, peer_of(right), ("g_left", step))
+        push(place, place, peer_of(left), ("g_right", step))
+        push(place, place, sib, ("s_own", step))
 
     for step, chip in enumerate((c, left, right, opp)):
         arrived(w2.at[chip, span((1 - k) * rows, rows)], ("wswap", step))
         arrived(w2.at[chip, span(k * rows, rows)], ("wkeep", step))
     update(0, lambda chip, r: x[pl.ds(pl.multiple_of(c * pair + r * step_rows, step_rows), step_rows), :])
     arrived(relay_c.at[0], "c_relay_l")
-    push(relay_c.at[0], back.at[left, pl.ds(0, rows)], peer_of(right), "c_opp_l")
+    push(relay_c.at[0], out.at[2 * left + k, own_rows(right, 0)], peer_of(right), "c_opp_l")
     arrived(relay_c.at[1], "c_relay_r")
-    push(relay_c.at[1], back.at[right, pl.ds(rows, rows)], peer_of(left), "c_opp_r")
+    push(relay_c.at[1], out.at[2 * right + k, own_rows(left, 1)], peer_of(left), "c_opp_r")
 
     def from_back(chip, r):
-        return back[chip, pl.ds(pl.multiple_of(r * step_rows, step_rows), step_rows), :]
-
-    arrived(back.at[left], "c_left")
+        return out[2 * chip + k, pl.ds(pl.multiple_of(c * pair + r * step_rows, step_rows), step_rows), :]
+
+    arrived(mine(left), "c_left")
     update(1, from_back)
-    arrived(back.at[right], "c_right")
+    arrived(mine(right), "c_right")
     update(2, from_back)
-    arrived(back.at[opp, pl.ds(0, rows)], "c_opp_l")
-    arrived(back.at[opp, pl.ds(rows, rows)], "c_opp_r")
+    arrived(mine(opp, 0, rows), "c_opp_l")
+    arrived(mine(opp, rows, rows), "c_opp_r")
     update(3, from_back)
 
     for step in range(chips):
@@ -247,7 +258,6 @@
         push(part_r, part_r, sib, ("s_far_r", step))
     for step in range(chips):
         mat = 2 * lax.rem(c + order[step], chips)
-        arrived(out.at[mat + k, own_rows(c)], ("own", step))
         arrived(out.at[mat + 1 - k, own_rows(c)], ("s_own", step))
         arrived(out.at[2 * lax.rem(left + order[step], chips) + 1 - k, own_rows(left)], ("s_left", step))
         arrived(out.at[2 * lax.rem(right + order[step], chips) + 1 - k, own_rows(right)], ("s_right", step))
@@ -255,7 +265,8 @@
         arrived(out.at[mat_o, own_rows(opp, 0)], ("s_far_l", step))
         arrived(out.at[mat_o, own_rows(opp, 1)], ("s_far_r", step))
     for copy in sent:
-        copy.wait_send()
+        if not any(copy is done for done in mine_sent):
+            copy.wait_send()
 
 
 def muon_step(group, low, sq_in, w):
@@ -266,27 +277,44 @@
     return pl.pallas_call(
         functools.partial(muon_kernel, group),
         in_specs=[hbm, pl.BlockSpec(memory_space=pltpu.VMEM), hbm],
-        out_specs=hbm,
-        out_shape=jax.ShapeDtypeStruct((mats, dim, cols), jnp.bfloat16),
+        out_specs=pl.BlockSpec(memory_space=pltpu.VMEM),
+        out_shape=pltpu.VMEM((mats, dim, cols), jnp.bfloat16),
         scratch_shapes=[
             pltpu.VMEM((dim, cols), jnp.bfloat16),
             pltpu.VMEM((dim, dim), jnp.bfloat16),
             pltpu.VMEM((dim, dim), jnp.bfloat16),
-            pltpu.VMEM((chips, pair, cols), jnp.bfloat16),
             pltpu.VMEM((2, rows, cols), jnp.bfloat16),
             pltpu.VMEM((2, rows, cols), jnp.bfloat16),
             pltpu.VMEM((chips, pair, cols), jnp.float32),
-            pltpu.VMEM((chips, pair, cols), jnp.bfloat16),
-            pltpu.VMEM((chips, pair, cols), jnp.bfloat16),
             pltpu.VMEM((group, 8, 128), jnp.float32),
             pltpu.SemaphoreType.DMA((80,)),
             pltpu.SemaphoreType.DMA((80,)),
             pltpu.SemaphoreType.REGULAR,
+            pltpu.SemaphoreType.REGULAR,
         ],
         compiler_params=pltpu.CompilerParams(
-            collective_id=0, has_side_effects=True, vmem_limit_bytes=58 * 1024 * 1024
+            collective_id=0, has_side_effects=True, vmem_limit_bytes=22 * 1024 * 1024
         ),
     )(low, sq_in, w)
+
+
+def store_kernel(src, dst, sem):
+    copies = [pltpu.make_async_copy(src.at[i], dst.at[i], sem.at[i]) for i in range(src.shape[0])]
+    for copy in copies:
+        copy.start()
+    for copy in copies:
+        copy.wait()
+
+
+def store_step(full):
+    return pl.pallas_call(
+        store_kernel,
+        in_specs=[pl.BlockSpec(memory_space=pltpu.VMEM)],
+        out_specs=pl.BlockSpec(memory_space=pl.ANY),
+        out_shape=jax.ShapeDtypeStruct(full.shape, full.dtype),
+        scratch_shapes=[pltpu.SemaphoreType.DMA((full.shape[0],))],
+        compiler_params=pltpu.CompilerParams(vmem_limit_bytes=1024 * 1024),
+    )(full)
 
 
 def solution(mesh):
@@ -296,7 +324,7 @@
 
     def local_step(w_rows, mom_rows, grad_rows):
         mom_new, low, square = momentum_step(mom_rows, grad_rows)
-        params = muon_step(group, low, square, w_rows)
+        params = store_step(muon_step(group, low, square, w_rows))
         return params, mom_new
 
     return jax.shard_map(

time: 335 us -> 322 us (0.961)
  local copies, waits for them, and re-layouts: 25.4 us -> 0 us
  Pallas kernels: 309 us -> 321 us
    unnamed x1 -> x0, local copies, waits for them, and re-layouts: 25.4 us -> none
    pallas_call x0 -> x1, Pallas kernels: none -> 12.3 us  [store_step(): pl.pallas_call(store_kernel, in_specs=[pl.BlockSpec(memory_space=pltpu.VM...]
where the time goes in v2:
time: 322 us
  Pallas kernels  321 us (100%)
    pallas_call x1, Pallas kernels, muon_step(): pl.pallas_call(functools.partial(muon_kernel, group), in_specs=[hbm, pl.B...  296 us
    pallas_call x1, Pallas kernels, momentum_step(): pl.pallas_call(momentum_kernel, grid=(mats,), in_specs=[block, block], ou...  12.6 us
    pallas_call x1, Pallas kernels, store_step(): pl.pallas_call(store_kernel, in_specs=[pl.BlockSpec(memory_space=pltpu.VM...  12.3 us

profile of v2, /device:TPU:81, one launch (start us, length us, event | category | flops | bytes accessed | tf_op | source)
XLA Modules:
  0.0 321.8 jit_solution(18295791332289019103)
XLA Ops:
  0.6 12.6 %shard_map.50 = (f32[8,96,3072]{2,1,0:T(8,128)}, bf16[8,96,3072]{2,1,0:T(8,128)(2,1)}, f32[8,8,128]{2,1,0:T(8,128)}) custom-call(f32[8,96,3072]{2,1,0:T(8,128)} %mom_ref.1, bf16[8,96,3072]{2,1,0:T(8,128)(2,1)} %grad_ref.1), custom_call_target="tpu_custom_call" | custom-call | tf_op jit(solution)/shard_map/pallas_call | solution.py:42
  13.2 296.3 %shard_map.51.src = bf16[8,768,3072]{2,1,0:T(8,128)(2,1)S(1)} custom-call(bf16[8,96,3072]{2,1,0:T(8,128)(2,1)} %get-tuple-element.5.low, f32[8,8,128]{2,1,0:T(8,128)} %get-tuple-element.6.sq_in, f32[8,96,3072]{2,1,0:T(8,128)} %w.1), custom_call_target="tpu_custom_call" | custom-call | tf_op jit(solution)/shard_map/pallas_call | solution.py:277
  309.5 12.3 %shard_map.52 = bf16[8,768,3072]{2,1,0:T(8,128)(2,1)} custom-call(bf16[8,768,3072]{2,1,0:T(8,128)(2,1)S(1)} %shard_map.51.src), custom_call_target="tpu_custom_call" | custom-call | tf_op jit(solution)/shard_map/pallas_call | solution.py:310

commit v3 on v0

v3 whole, which is shorter than its diff:
```python
import functools
import math

import jax
import jax.numpy as jnp
from jax import lax
from jax.experimental import pallas as pl
from jax.experimental.pallas import tpu as pltpu
from jax.sharding import PartitionSpec as P

NS_ITERS = 5
MOMENTUM = 0.95
LEARN_RATE = 0.02
WEIGHT_DECAY = 0.1
NORM_EPS = 1e-7
COEF_A = 3.4445
COEF_B = -4.7750
COEF_C = 2.0315

MESH = pl.DeviceIdType.MESH
TILE = 256
WIDE = 1024
SCALE_ROWS = 32
STEP_ROWS = 16


def ds(start, size):
    return pl.ds(pl.multiple_of(start, math.gcd(size, TILE)), size)


def symmetric(dst, product, finish, dim):
    for j in range(0, dim, TILE):
        cols = slice(j, j + TILE)
        block = finish(product(slice(j, dim), cols), slice(j, dim), cols)
        dst[j:, cols] = block
        for i in range(j + TILE, dim, TILE):
            dst[cols, i : i + TILE] = block[i - j : i - j + TILE].T


def newton_schulz_poly(x, gram, poly):
    dim = gram.shape[0]

    def outer(rows, cols):
        return lax.dot_general(x[rows, :], x[cols, :], (((1,), (1,)), ((), ())), preferred_element_type=jnp.float32)

    def square(rows, cols):
        return jnp.dot(gram[rows, :], gram[:, cols], preferred_element_type=jnp.float32)

    symmetric(gram, outer, lambda prod, rows, cols: prod.astype(jnp.bfloat16), dim)
    symmetric(
        poly,
        square,
        lambda prod, rows, cols: (COEF_B * gram[rows, cols].astype(jnp.float32) + COEF_C * prod).astype(jnp.bfloat16),
        dim,
    )


def newton_schulz_step(x, poly, part):
    old = x[:, part]
    prod = jnp.dot(poly[...], old, preferred_element_type=jnp.float32)
    x[:, part] = (COEF_A * old.astype(jnp.float32) + prod).astype(jnp.bfloat16)


def muon_kernel(group, mom, grad, w, out, mom_new, w_sib, x, gram, poly, relay, w_buf, sq, send, recv, go, free):
    chips = group // 2
    mats, rows, cols = mom.shape
    pair = 2 * rows
    dim = pair * chips
    rms_scale = 0.2 * math.sqrt(max(dim, cols))
    me = lax.axis_index("data")
    c, k = lax.div(me, 2), lax.rem(me, 2)
    sib = 2 * c + 1 - k
    right, left, opp = (lax.rem(c + step, chips) for step in (1, chips - 1, 2))

    def peer_of(chip):
        return 2 * chip + k

    def own_rows(chip, half=None):
        if half is None:
            return ds(chip * pair, pair)
        return ds(chip * pair + half * rows, rows)

    def mine(chip, half=None):
        return out.at[2 * chip + k, own_rows(c, half)]

    sent, slots = [], {}

    def slot(key):
        return slots.setdefault(key, len(slots))

    def remote(src, dst, peer, key):
        copy = pltpu.make_async_remote_copy(
            src_ref=src, dst_ref=dst, send_sem=send.at[len(sent)], recv_sem=recv.at[slot(key)],
            device_id={"data": peer}, device_id_type=MESH)
        sent.append(copy)
        return copy

    def push(src, dst, peer, key):
        copy = remote(src, dst, peer, key)
        copy.start()
        return copy

    def load(src, dst, key):
        pltpu.make_async_copy(src, dst, recv.at[slot(key)]).start()

    def arrived(dst, key):
        pltpu.make_async_copy(dst, dst, recv.at[slot(key)]).wait()

    steps = (opp, right, left, c)
    for step, chip in enumerate(steps):
        for par in range(2):
            load(mom.at[2 * chip + par], mom_new.at[2 * chip + par], ("mom", step, par))
            load(grad.at[2 * chip + par], out.at[2 * chip + k, own_rows(left, par)], ("grad", step, par))

    barrier = pltpu.get_barrier_semaphore()
    for step in range(1, group):
        pl.semaphore_signal(barrier, inc=1, device_id={"data": lax.rem(me + step, group)}, device_id_type=MESH)
    pl.semaphore_wait(barrier, group - 1)

    def momentum(step, chip, par):
        mat = 2 * chip + par
        base = jnp.where(k == par, c * pair + k * rows, right * pair)
        arrived(mom_new.at[mat], ("mom", step, par))
        arrived(out.at[2 * chip + k, own_rows(left, par)], ("grad", step, par))

        def body(r, total):
            part = ds(r * STEP_ROWS, STEP_ROWS)
            low = out[2 * chip + k, ds(left * pair + par * rows + r * STEP_ROWS, STEP_ROWS), :]
            new = MOMENTUM * mom_new[mat, part, :] + low.astype(jnp.float32)
            mom_new[mat, part, :] = new
            out[2 * chip + k, ds(base + r * STEP_ROWS, STEP_ROWS), :] = new.astype(jnp.bfloat16)
            square = new * new
            lanes = square[:, :128]
            for start in range(128, cols, 128):
                lanes = lanes + square[:, start : start + 128]
            for start in range(0, STEP_ROWS, 8):
                total = total + lanes[start : start + 8]
            return total

        sq[0, mat] = lax.fori_loop(0, rows // STEP_ROWS, body, jnp.zeros((8, 128), jnp.float32))

    swap = [
        remote(out.at[2 * chip + k, own_rows(right, 0)], out.at[2 * chip + 1 - k, own_rows(c, k)], sib, ("swap", step))
        for step, chip in enumerate(steps)
    ]
    exchange = [
        [
            remote(mine(opp, 0), relay.at[0], peer_of(right), "a_relay_l"),
            remote(mine(opp, 1), relay.at[1], peer_of(left), "a_relay_r"),
        ],
        [remote(mine(right), x.at[own_rows(c)], peer_of(right), "a_left")],
        [remote(mine(left), x.at[own_rows(c)], peer_of(left), "a_right")],
        [],
    ]

    def send_rows(step, chip):
        arrived(mine(chip, 1 - k), ("swap", step))
        for copy in exchange[step]:
            copy.start()

    for step, chip in enumerate(steps):
        momentum(step, chip, 0)

        @pl.when(k == 1)
        def _():
            swap[step].start()

        @pl.when(k == 0)
        def _():
            send_rows(step, chip)

    for step, chip in enumerate(steps):
        momentum(step, chip, 1)

        @pl.when(k == 0)
        def _():
            swap[step].start()

    for step in range(1, group):
        dest = lax.rem(me + step, group)
        push(sq.at[0, dest], sq.at[1, step], dest, ("sq", step))
    for step, chip in enumerate((c, left, right, opp)):
        push(w.at[2 * chip + 1 - k], w_sib.at[chip], sib, ("w_swap", step))

    @pl.when(k == 1)
    def _():
        pl.semaphore_wait(go, 1)
        for step, chip in enumerate(steps):
            send_rows(step, chip)

    arrived(relay.at[0], "a_relay_l")
    pass_right = push(relay.at[0], x.at[own_rows(left, 0)], peer_of(right), "a_opp_l")
    arrived(relay.at[1], "a_relay_r")
    pass_left = push(relay.at[1], x.at[own_rows(right, 1)], peer_of(left), "a_opp_r")

    total = sq[0, me]
    for step in range(1, group):
        arrived(sq.at[1, step], ("sq", step))
        total = total + sq[1, step]
    norm = jnp.sqrt(jnp.sum(total, keepdims=True))
    inverse = 1.0 / (norm + NORM_EPS)

    def scale(get, base):
        @pl.loop(0, pair // SCALE_ROWS)
        def _(r):
            part = ds(base + r * SCALE_ROWS, SCALE_ROWS)
            x[part, :] = (get(part).astype(jnp.float32) * inverse).astype(jnp.bfloat16)

    scale(lambda part: out[2 * c + k, part, :], c * pair)
    arrived(x.at[own_rows(left)], "a_left")
    scale(lambda part: x[part, :], left * pair)
    arrived(x.at[own_rows(right)], "a_right")
    scale(lambda part: x[part, :], right * pair)
    arrived(x.at[own_rows(opp, 0)], "a_opp_l")
    arrived(x.at[own_rows(opp, 1)], "a_opp_r")

    @pl.when(k == 0)
    def _():
        pl.semaphore_signal(go, inc=1, device_id={"data": sib}, device_id_type=MESH)

    scale(lambda part: x[part, :], opp * pair)

    waited = swap + sum(exchange, []) + [pass_right, pass_left]
    for copy in waited:
        copy.wait_send()
    for chip in (right, left):
        pl.semaphore_signal(free, inc=1, device_id={"data": peer_of(chip)}, device_id_type=MESH)

    order = (c, left, right, opp)

    def load_w(step):
        load(w.at[2 * order[step] + k], w_buf.at[step % 2, ds(k * rows, rows)], ("w_own", step))
        arrived(w_sib.at[order[step]], ("w_swap", step))
        load(w_sib.at[order[step]], w_buf.at[step % 2, ds((1 - k) * rows, rows)], ("w_sib", step))

    load_w(0)
    load_w(1)

    @pl.loop(0, NS_ITERS - 1)
    def _(_):
        newton_schulz_poly(x, gram, poly)

        @pl.loop(0, cols // WIDE)
        def _(j):
            newton_schulz_step(x, poly, ds(j * WIDE, WIDE))

    newton_schulz_poly(x, gram, poly)
    pl.semaphore_wait(free, 2)

    chunks = [pl.ds(start, WIDE) for start in range(0, cols, WIDE)]
    for n, part in enumerate(chunks):
        newton_schulz_step(x, poly, part)
        push(x.at[own_rows(opp, 0), part], relay.at[0, :, part], peer_of(right), ("c_relay_l", n))
        push(x.at[own_rows(opp, 1), part], relay.at[1, :, part], peer_of(left), ("c_relay_r", n))
        push(x.at[own_rows(right), part], out.at[2 * c + k, own_rows(right), part], peer_of(right), ("c_left", n))
        push(x.at[own_rows(left), part], out.at[2 * c + k, own_rows(left), part], peer_of(left), ("c_right", n))

    def update(step, get):
        chip = order[step]
        arrived(w_buf.at[step % 2, ds(k * rows, rows)], ("w_own", step))
        arrived(w_buf.at[step % 2, ds((1 - k) * rows, rows)], ("w_sib", step))

        @pl.loop(0, pair // STEP_ROWS)
        def _(r):
            w_part = w_buf[step % 2, ds(r * STEP_ROWS, STEP_ROWS), :]
            part = ds(c * pair + r * STEP_ROWS, STEP_ROWS)
            ortho = get(chip, part).astype(jnp.float32) * rms_scale
            out[2 * chip + k, part, :] = (w_part - LEARN_RATE * (ortho + WEIGHT_DECAY * w_part)).astype(jnp.bfloat16)

        if step + 2 < chips:
            load_w(step + 2)
        push(mine(chip), mine(chip), peer_of(right), ("g_left", step))
        push(mine(chip), mine(chip), peer_of(left), ("g_right", step))
        push(mine(chip), mine(chip), sib, ("s_own", step))

    update(0, lambda chip, part: x[part, :])
    for n, part in enumerate(chunks):
        arrived(relay.at[0, :, part], ("c_relay_l", n))
        push(relay.at[0, :, part], out.at[2 * left + k, own_rows(right, 0), part], peer_of(right), ("c_opp_l", n))
        arrived(relay.at[1, :, part], ("c_relay_r", n))
        push(relay.at[1, :, part], out.at[2 * right + k, own_rows(left, 1), part], peer_of(left), ("c_opp_r", n))

    def returned(chip, part):
        return out[2 * chip + k, part, :]

    def x_rows(chip, half, part):
        return out.at[2 * chip + k, own_rows(c, half), part]

    for n, part in enumerate(chunks):
        arrived(x_rows(left, None, part), ("c_left", n))
    update(1, returned)
    for n, part in enumerate(chunks):
        arrived(x_rows(right, None, part), ("c_right", n))
    update(2, returned)
    for n, part in enumerate(chunks):
        arrived(x_rows(opp, 0, part), ("c_opp_l", n))
        arrived(x_rows(opp, 1, part), ("c_opp_r", n))
    update(3, returned)

    def near(chip, step):
        return lax.rem(chip + (0, chips - 1, 1, 2)[step], chips)

    for step in range(chips):
        mat_l, mat_r = 2 * near(left, step) + k, 2 * near(right, step) + k
        whole_l, whole_r = out.at[mat_l, own_rows(left)], out.at[mat_r, own_rows(right)]
        part_l, part_r = out.at[mat_l, own_rows(left, 0)], out.at[mat_r, own_rows(right, 1)]
        arrived(whole_l, ("g_left", step))
        push(part_l, part_l, peer_of(right), ("f_left", step))
        push(whole_l, whole_l, sib, ("s_left", step))
        arrived(whole_r, ("g_right", step))
        push(part_r, part_r, peer_of(left), ("f_right", step))
        push(whole_r, whole_r, sib, ("s_right", step))
    for step in range(chips):
        mat = 2 * near(opp, step) + k
        part_l, part_r = out.at[mat, own_rows(opp, 0)], out.at[mat, own_rows(opp, 1)]
        arrived(part_l, ("f_left", step))
        push(part_l, part_l, sib, ("s_far_l", step))
        arrived(part_r, ("f_right", step))
        push(part_r, part_r, sib, ("s_far_r", step))
    for step in range(chips):
        arrived(out.at[2 * near(c, step) + 1 - k, own_rows(c)], ("s_own", step))
        arrived(out.at[2 * near(left, step) + 1 - k, own_rows(left)], ("s_left", step))
        arrived(out.at[2 * near(right, step) + 1 - k, own_rows(right)], ("s_right", step))
        arrived(out.at[2 * near(opp, step) + 1 - k, own_rows(opp, 0)], ("s_far_l", step))
        arrived(out.at[2 * near(opp, step) + 1 - k, own_rows(opp, 1)], ("s_far_r", step))
    for copy in sent:
        if not any(copy is done for done in waited):
            copy.wait_send()


def muon_step(group, mom, grad, w):
    mats, rows, cols = mom.shape
    chips, pair = group // 2, 2 * rows
    dim = pair * chips
    hbm = pl.BlockSpec(memory_space=pl.ANY)
    vmem = pl.BlockSpec(memory_space=pltpu.VMEM)
    return pl.pallas_call(
        functools.partial(muon_kernel, group),
        in_specs=[hbm, hbm, hbm],
        out_specs=[vmem, vmem, hbm],
        out_shape=[
            pltpu.VMEM((mats, dim, cols), jnp.bfloat16),
            pltpu.VMEM((mats, rows, cols), jnp.float32),
            pltpu.HBM((chips, rows, cols), jnp.float32),
        ],
        scratch_shapes=[
            pltpu.VMEM((dim, cols), jnp.bfloat16),
            pltpu.VMEM((dim, dim), jnp.bfloat16),
            pltpu.VMEM((dim, dim), jnp.bfloat16),
            pltpu.VMEM((2, rows, cols), jnp.bfloat16),
            pltpu.VMEM((2, pair, cols), jnp.float32),
            pltpu.VMEM((2, group, 8, 128), jnp.float32),
            pltpu.SemaphoreType.DMA((128,)),
            pltpu.SemaphoreType.DMA((128,)),
            pltpu.SemaphoreType.REGULAR,
            pltpu.SemaphoreType.REGULAR,
        ],
        compiler_params=pltpu.CompilerParams(
            collective_id=0, has_side_effects=True, vmem_limit_bytes=15 * 1024 * 1024
        ),
    )(mom, grad, w)


def store_kernel(src, dst, sem):
    copies = [pltpu.make_async_copy(src.at[i], dst.at[i], sem.at[i]) for i in range(src.shape[0])]
    for copy in copies:
        copy.start()
    for copy in copies:
        copy.wait()


def store_step(full):
    return pl.pallas_call(
        store_kernel,
        in_specs=[pl.BlockSpec(memory_space=pltpu.VMEM)],
        out_specs=pl.BlockSpec(memory_space=pl.ANY),
        out_shape=jax.ShapeDtypeStruct(full.shape, full.dtype),
        scratch_shapes=[pltpu.SemaphoreType.DMA((full.shape[0],))],
        compiler_params=pltpu.CompilerParams(vmem_limit_bytes=1024 * 1024),
    )(full)


def solution(mesh):
    group = mesh.shape["data"]
    row_spec = P("stage", "data", None)
    full_spec = P("stage", None, None)

    def local_step(w_rows, mom_rows, grad_rows):
        params, mom_new, _ = muon_step(group, mom_rows, grad_rows, w_rows)
        return store_step(params), store_step(mom_new)

    return jax.shard_map(
        local_step, mesh=mesh, in_specs=(row_spec, row_spec, row_spec), out_specs=(full_spec, row_spec), check_vma=False
    )
```

time: 537 us -> 297 us (0.55)
  Pallas kernels: 0 us -> 297 us
  waiting for transfers between devices: 175 us -> 0 us
  blocking collectives: 119 us -> 0 us
  matrix products: 85.4 us -> 0 us
  other arithmetic: 67.5 us -> 0 us
  local copies, waits for them, and re-layouts: 65.2 us -> 0 us
  between operations: 15 us -> 0.65 us
  starting transfers between devices: 6.51 us -> 0 us
    pallas_call x0 -> x3, Pallas kernels: none -> 297 us  [the longest x1 280 us: muon_step(): pl.pallas_call(functools.partial(muon_kernel, group), in_specs=[hbm, hbm,...]
    all_gather x1 -> x0, waiting for transfers between devices: 175 us -> none  [local_step(): lax.all_gather(w_new.astype(jnp.bfloat16), 'data', axis=1, tiled=True)]
    dot_general x10 -> x0, matrix products: 85.4 us -> none  [the longest x5 50.9 us: newton_schulz(): jnp.einsum('kij,kjp->kip', poly_mat, x_mat, preferred_element_type=jnp.fl...]
    all_to_all x1 -> x0, blocking collectives: 60.4 us -> none  [local_step(): ortho_rows = lax.all_to_all(x_mat, 'data', 1, 0, tiled=True)]
    psum x1 -> x0, blocking collectives: 58.7 us -> none  [local_step(): sq_total = lax.psum(jnp.sum(mom_new * mom_new, axis=(1, 2)), 'data')]
    unnamed x9 -> x0, local copies, waits for them, and re-layouts: 55.1 us -> none
    unnamed x1 -> x0, other arithmetic: 28.8 us -> none
    convert_element_type x3 -> x0, other arithmetic: 17.3 us -> none  [the longest x1 11 us: local_step(): w_new.astype(jnp.bfloat16)]
  transfers between devices with their start and end apart: 2 -> 0, of which waited for: 1 -> 0; matrix products, arithmetic and copies ran while one was open for 0% -> 0% of each run, Pallas kernels for 0% -> 0%
where the time goes in v3:
time: 297 us
  Pallas kernels  297 us (100%)
    pallas_call x1, Pallas kernels, muon_step(): pl.pallas_call(functools.partial(muon_kernel, group), in_specs=[hbm, hbm,...  280 us
    pallas_call x2, Pallas kernels, store_step(): pl.pallas_call(store_kernel, in_specs=[pl.BlockSpec(memory_space=pltpu.VM...  16 us

profile of v3, /device:TPU:81, one launch (start us, length us, event | category | flops | bytes accessed | tf_op | source)
XLA Modules:
  0.0 297.2 jit_solution(4737873441664264341)
XLA Ops:
  0.6 280.5 %shard_map.50 = (bf16[8,768,3072]{2,1,0:T(8,128)(2,1)S(1)}, f32[8,96,3072]{2,1,0:T(8,128)S(1)}, f32[4,96,3072]{2,1,0:T(8,128)}) custom-call(f32[8,96,3072]{2,1,0:T(8,128)} %mom.1, bf16[8,96,3072]{2,1,0:T(8,128)(2,1)} %grad.1, f32[8,96,3072]{2,1,0:T(8,128)} %w.1), custom_call_target="tpu_custom_call" | custom-call | tf_op jit(solution)/shard_map/pallas_call | solution.py:337
  281.1 12.3 %shard_map.51 = bf16[8,768,3072]{2,1,0:T(8,128)(2,1)} custom-call(bf16[8,768,3072]{2,1,0:T(8,128)(2,1)S(1)} %get-tuple-element.4.src), custom_call_target="tpu_custom_call" | custom-call | tf_op jit(solution)/shard_map/pallas_call | solution.py:373
  293.5 3.7 %shard_map.52 = f32[8,96,3072]{2,1,0:T(8,128)} custom-call(f32[8,96,3072]{2,1,0:T(8,128)S(1)} %get-tuple-element.5.src), custom_call_target="tpu_custom_call" | custom-call | tf_op jit(solution)/shard_map/pallas_call | solution.py:373

commit v4 on v3

--- a/solution.py
+++ b/solution.py
@@ -61,7 +61,7 @@
     x[:, part] = (COEF_A * old.astype(jnp.float32) + prod).astype(jnp.bfloat16)
 
 
-def muon_kernel(group, mom, grad, w, out, mom_new, w_sib, x, gram, poly, relay, w_buf, sq, send, recv, go, free):
+def muon_kernel(group, mom, grad, w, out, mom_new, w_sib, tail_r, tail_l, x, gram, poly, relay, w_buf, sq, send, recv, go, free):
     chips = group // 2
     mats, rows, cols = mom.shape
     pair = 2 * rows
@@ -239,10 +239,7 @@
     @pl.loop(0, NS_ITERS - 1)
     def _(_):
         newton_schulz_poly(x, gram, poly)
-
-        @pl.loop(0, cols // WIDE)
-        def _(j):
-            newton_schulz_step(x, poly, ds(j * WIDE, WIDE))
+        newton_schulz_step(x, poly, pl.ds(0, cols))
 
     newton_schulz_poly(x, gram, poly)
     pl.semaphore_wait(free, 2)
@@ -300,17 +297,24 @@
     def near(chip, step):
         return lax.rem(chip + (0, chips - 1, 1, 2)[step], chips)
 
+    last = chips - 1
     for step in range(chips):
         mat_l, mat_r = 2 * near(left, step) + k, 2 * near(right, step) + k
         whole_l, whole_r = out.at[mat_l, own_rows(left)], out.at[mat_r, own_rows(right)]
         part_l, part_r = out.at[mat_l, own_rows(left, 0)], out.at[mat_r, own_rows(right, 1)]
         arrived(whole_l, ("g_left", step))
-        push(part_l, part_l, peer_of(right), ("f_left", step))
+        if step < last:
+            push(part_l, part_l, peer_of(right), ("f_left", step))
+        else:
+            load(part_l, tail_r, "tail_r")
         push(whole_l, whole_l, sib, ("s_left", step))
         arrived(whole_r, ("g_right", step))
-        push(part_r, part_r, peer_of(left), ("f_right", step))
+        if step < last:
+            push(part_r, part_r, peer_of(left), ("f_right", step))
+        else:
+            load(part_r, tail_l, "tail_l")
         push(whole_r, whole_r, sib, ("s_right", step))
-    for step in range(chips):
+    for step in range(last):
         mat = 2 * near(opp, step) + k
         part_l, part_r = out.at[mat, own_rows(opp, 0)], out.at[mat, own_rows(opp, 1)]
         arrived(part_l, ("f_left", step))
@@ -321,8 +325,11 @@
         arrived(out.at[2 * near(c, step) + 1 - k, own_rows(c)], ("s_own", step))
         arrived(out.at[2 * near(left, step) + 1 - k, own_rows(left)], ("s_left", step))
         arrived(out.at[2 * near(right, step) + 1 - k, own_rows(right)], ("s_right", step))
-        arrived(out.at[2 * near(opp, step) + 1 - k, own_rows(opp, 0)], ("s_far_l", step))
-        arrived(out.at[2 * near(opp, step) + 1 - k, own_rows(opp, 1)], ("s_far_r", step))
+        if step < last:
+            arrived(out.at[2 * near(opp, step) + 1 - k, own_rows(opp, 0)], ("s_far_l", step))
+            arrived(out.at[2 * near(opp, step) + 1 - k, own_rows(opp, 1)], ("s_far_r", step))
+    arrived(tail_r, "tail_r")
+    arrived(tail_l, "tail_l")
     for copy in sent:
         if not any(copy is done for done in waited):
             copy.wait_send()
@@ -337,11 +344,13 @@
     return pl.pallas_call(
         functools.partial(muon_kernel, group),
         in_specs=[hbm, hbm, hbm],
-        out_specs=[vmem, vmem, hbm],
+        out_specs=[vmem, vmem, hbm, hbm, hbm],
         out_shape=[
             pltpu.VMEM((mats, dim, cols), jnp.bfloat16),
             pltpu.VMEM((mats, rows, cols), jnp.float32),
             pltpu.HBM((chips, rows, cols), jnp.float32),
+            pltpu.HBM((rows, cols), jnp.bfloat16),
+            pltpu.HBM((rows, cols), jnp.bfloat16),
         ],
         scratch_shapes=[
             pltpu.VMEM((dim, cols), jnp.bfloat16),
@@ -377,7 +386,43 @@
         out_shape=jax.ShapeDtypeStruct(full.shape, full.dtype),
         scratch_shapes=[pltpu.SemaphoreType.DMA((full.shape[0],))],
         compiler_params=pltpu.CompilerParams(vmem_limit_bytes=1024 * 1024),
+        cost_estimate=pl.CostEstimate(flops=1000 * full.size, bytes_accessed=2 * full.size, transcendentals=0),
     )(full)
+
+
+def tail_kernel(params, near_l, near_r, far_l, far_r, out, buf, sem):
+    rows = buf.shape[1]
+    pair = 2 * rows
+    chips = params.shape[1] // pair
+    me = lax.axis_index("data")
+    c, k = lax.div(me, 2), lax.rem(me, 2)
+    start = lax.rem(c + 2, chips) * pair
+    pieces = ((near_l, k, 0), (near_r, k, 1), (far_l, 1 - k, 0), (far_r, 1 - k, 1))
+    loads = [pltpu.make_async_copy(src, buf.at[n], sem.at[n]) for n, (src, _, _) in enumerate(pieces)]
+    stores = [
+        pltpu.make_async_copy(buf.at[n], out.at[2 * c + par, pl.ds(pl.multiple_of(start + half * rows, rows), rows)], sem.at[n])
+        for n, (_, par, half) in enumerate(pieces)
+    ]
+    for copy in loads:
+        copy.start()
+    for copy, store in zip(loads, stores):
+        copy.wait()
+        store.start()
+    for store in stores:
+        store.wait()
+
+
+def tail_step(params, pieces):
+    hbm = pl.BlockSpec(memory_space=pl.ANY)
+    return pl.pallas_call(
+        tail_kernel,
+        in_specs=[hbm] * 5,
+        out_specs=hbm,
+        out_shape=jax.ShapeDtypeStruct(params.shape, params.dtype),
+        input_output_aliases={0: 0},
+        scratch_shapes=[pltpu.VMEM((4, *pieces[0].shape), pieces[0].dtype), pltpu.SemaphoreType.DMA((4,))],
+        compiler_params=pltpu.CompilerParams(vmem_limit_bytes=4 * 1024 * 1024),
+    )(params, *pieces)
 
 
 def solution(mesh):
@@ -386,8 +431,17 @@
     full_spec = P("stage", None, None)
 
     def local_step(w_rows, mom_rows, grad_rows):
-        params, mom_new, _ = muon_step(group, mom_rows, grad_rows, w_rows)
-        return store_step(params), store_step(mom_new)
+        params, mom_new, _, tail_r, tail_l = muon_step(group, mom_rows, grad_rows, w_rows)
+        to_right = [(d, (d + 2) % group) for d in range(group)]
+        to_left = [(d, (d - 2) % group) for d in range(group)]
+        swap = [(d, d + 1 - 2 * (d % 2)) for d in range(group)]
+        near = [lax.ppermute(tail_r, "data", to_right), lax.ppermute(tail_l, "data", to_left)]
+        params = store_step(params)
+        *near, params = lax.optimization_barrier((*near, params))
+        far = [lax.ppermute(piece, "data", swap) for piece in near]
+        mom_new = store_step(mom_new)
+        *far, mom_new = lax.optimization_barrier((*far, mom_new))
+        return tail_step(params, near + far), mom_new
 
     return jax.shard_map(
         local_step, mesh=mesh, in_specs=(row_spec, row_spec, row_spec), out_specs=(full_spec, row_spec), check_vma=False

time: 297 us -> 289 us (0.973)
  Pallas kernels: 297 us -> 284 us
  starting transfers between devices: 0 us -> 4.09 us
    pallas_call x1, Pallas kernels: 280 us -> 266 us  [muon_step(): pl.pallas_call(functools.partial(muon_kernel, group), in_specs=[hbm, hbm,...]
    ppermute x0 -> x4, starting transfers between devices: none -> 4.09 us  [the longest x1 2.65 us: local_step(): lax.ppermute(tail_l, 'data', to_left)]
  transfers between devices with their start and end apart: 0 -> 4, of which waited for: 0 -> 1; matrix products, arithmetic and copies ran while one was open for 0% -> 0% of each run, Pallas kernels for 0% -> 6%
where the time goes in v4:
time: 289 us
  Pallas kernels  284 us (98%)
  starting transfers between devices  4.09 us (1%)
    pallas_call x1, Pallas kernels, muon_step(): pl.pallas_call(functools.partial(muon_kernel, group), in_specs=[hbm, hbm,...  266 us
    pallas_call x2, Pallas kernels, store_step(): pl.pallas_call(store_kernel, in_specs=[pl.BlockSpec(memory_space=pltpu.VM...  16 us
  transfers between devices with their start and end apart: 4, of which 1 were waited for; matrix products, arithmetic and copies ran while one was open for 0% of the time, Pallas kernels for 6%

profile of v4, /device:TPU:81, one launch (start us, length us, event | category | flops | bytes accessed | tf_op | source)
XLA Modules:
  0.0 289.2 jit_solution(17050036559080336587)
XLA Ops:
  0.6 265.9 %shard_map.50 = (bf16[8,768,3072]{2,1,0:T(8,128)(2,1)S(1)}, f32[8,96,3072]{2,1,0:T(8,128)S(1)}, f32[4,96,3072]{2,1,0:T(8,128)}, bf16[96,3072]{1,0:T(8,128)(2,1)}, bf16[96,3072]{1,0:T(8,128)(2,1)}) custom-call(f32[8,96,3072]{2,1,0:T(8,128)} %mom.1, bf16[8,96,3072]{2,1,0:T(8,128)(2,1)} %grad.1, f32[8,96,3072]{2,1,0:T(8,128)} %w.1), custom_call_target="tpu_custom_call" | custom-call | tf_op jit(solution)/shard_map/pallas_call | solution.py:344
  266.5 0.1 collective-permute-start
  266.6 2.7 collective-permute-start.1
  269.3 12.3 %shard_map.51.params = bf16[8,768,3072]{2,1,0:T(8,128)(2,1)} custom-call(bf16[8,768,3072]{2,1,0:T(8,128)(2,1)S(1)} %get-tuple-element.14.src), custom_call_target="tpu_custom_call" | custom-call | flops 18874368000 | bytes 37748736 | tf_op jit(solution)/shard_map/pallas_call | solution.py:382
  281.6 0.6 collective-permute-done.near_l
  282.2 0.0 collective-permute-done.1.near_r
  282.2 1.3 collective-permute-start.2
  283.5 0.0 collective-permute-start.3
  283.6 3.7 %shard_map.52 = f32[8,96,3072]{2,1,0:T(8,128)} custom-call(f32[8,96,3072]{2,1,0:T(8,128)S(1)} %get-tuple-element.18.src), custom_call_target="tpu_custom_call" | custom-call | flops 2359296000 | bytes 4718592 | tf_op jit(solution)/shard_map/pallas_call | solution.py:382
  287.3 0.0 collective-permute-done.2.far_l
  287.3 0.0 collective-permute-done.3.far_r
  287.3 1.9 shard_map.53
Async XLA Ops:
  266.5 15.7 %collective-permute-start = (bf16[96,3072]{1,0:T(8,128)(2,1)}, bf16[96,3072]{1,0:T(8,128)(2,1)S(1)}, u32[]{:S(2)}, u32[]{:S(2)}) collective-permute-start(bf16[96,3072]{1,0:T(8,128)(2,1)} %get-tuple-element.12), channel_id=1, source_target_pairs={{0,2},{1,3},{2,4},{3,5},{4,6},{5,7},{6,0},{7,1},{8,10},{9,11},{10,... | collective-permute-start | bytes 1769480 | tf_op jit(solution)/shard_map/ppermute | solution.py:438
  266.6 15.6 %collective-permute-start.1 = (bf16[96,3072]{1,0:T(8,128)(2,1)}, bf16[96,3072]{1,0:T(8,128)(2,1)S(1)}, u32[]{:S(2)}, u32[]{:S(2)}) collective-permute-start(bf16[96,3072]{1,0:T(8,128)(2,1)} %get-tuple-element.13), channel_id=1, source_target_pairs={{0,6},{1,7},{2,0},{3,1},{4,2},{5,3},{6,4},{7,5},{8,14},{9,15},{10,... | collective-permute-start | bytes 1769480 | tf_op jit(solution)/shard_map/ppermute | solution.py:438
  282.2 5.0 %collective-permute-start.2 = (bf16[96,3072]{1,0:T(8,128)(2,1)S(1)}, bf16[96,3072]{1,0:T(8,128)(2,1)S(1)}, u32[]{:S(2)}, u32[]{:S(2)}) collective-permute-start(bf16[96,3072]{1,0:T(8,128)(2,1)S(1)} %collective-permute-done.near_l), channel_id=1, source_target_pairs={{0,1},{1,0},{2,3},{3,2},{4,5},{5,4},{6,7},{7,6},{8,9},{9,8},{10,11... | collective-permute-start | bytes 1769480 | tf_op jit(solution)/shard_map/ppermute | solution.py:441
  283.5 3.7 %collective-permute-start.3 = (bf16[96,3072]{1,0:T(8,128)(2,1)S(1)}, bf16[96,3072]{1,0:T(8,128)(2,1)S(1)}, u32[]{:S(2)}, u32[]{:S(2)}) collective-permute-start(bf16[96,3072]{1,0:T(8,128)(2,1)S(1)} %collective-permute-done.1.near_r), channel_id=1, source_target_pairs={{0,1},{1,0},{2,3},{3,2},{4,5},{5,4},{6,7},{7,6},{8,9},{9,8},{10,11... | collective-permute-start | bytes 1769480 | tf_op jit(solution)/shard_map/ppermute | solution.py:441

commit v5 on v4

--- a/solution.py
+++ b/solution.py
@@ -25,7 +25,7 @@
 
 
 def ds(start, size):
-    return pl.ds(pl.multiple_of(start, math.gcd(size, TILE)), size)
+    return pl.ds(pl.multiple_of(start, math.gcd(size, STEP_ROWS)), size)
 
 
 def symmetric(dst, product, finish, dim):
@@ -61,7 +61,7 @@
     x[:, part] = (COEF_A * old.astype(jnp.float32) + prod).astype(jnp.bfloat16)
 
 
-def muon_kernel(group, mom, grad, w, out, mom_new, w_sib, tail_r, tail_l, x, gram, poly, relay, w_buf, sq, send, recv, go, free):
+def muon_kernel(group, mom, grad, w, out, mom_new, w_sib, tail_r, tail_l, x, gram, poly, relay, w_buf, w_ahead, sq, send, recv, go, free):
     chips = group // 2
     mats, rows, cols = mom.shape
     pair = 2 * rows
@@ -79,6 +79,25 @@
         if half is None:
             return ds(chip * pair, pair)
         return ds(chip * pair + half * rows, rows)
+
+    ahead = rows // 2
+    ahead_start, rest_start, rest = k * (pair - ahead), (1 - k) * ahead, pair - ahead
+
+    def ahead_rows(chip):
+        return ds(chip * pair + ahead_start, ahead)
+
+    def rest_rows(chip):
+        return ds(chip * pair + rest_start, rest)
+
+    split = STEP_ROWS * (rest // STEP_ROWS // 2)
+    sizes = ((rows, rows), (rest - split, split), (split, rest - split), (rows, rows))
+
+    def block(chip, step):
+        return rest_rows(chip) if step in (1, 2) else own_rows(chip)
+
+    def block_part(chip, step, way):
+        start = rest_start if step in (1, 2) else 0
+        return ds(chip * pair + start + way * sizes[step][0], sizes[step][way])
 
     def mine(chip, half=None):
         return out.at[2 * chip + k, own_rows(c, half)]
@@ -192,6 +211,8 @@
     pass_right = push(relay.at[0], x.at[own_rows(left, 0)], peer_of(right), "a_opp_l")
     arrived(relay.at[1], "a_relay_r")
     pass_left = push(relay.at[1], x.at[own_rows(right, 1)], peer_of(left), "a_opp_r")
+    push(w.at[2 * right + k, ds(k * ahead, ahead)], w_ahead.at[0], peer_of(right), "w_ahead_l")
+    push(w.at[2 * left + k, ds(k * ahead, ahead)], w_ahead.at[1], peer_of(left), "w_ahead_r")
 
     total = sq[0, me]
     for step in range(1, group):
@@ -249,28 +270,45 @@
         newton_schulz_step(x, poly, part)
         push(x.at[own_rows(opp, 0), part], relay.at[0, :, part], peer_of(right), ("c_relay_l", n))
         push(x.at[own_rows(opp, 1), part], relay.at[1, :, part], peer_of(left), ("c_relay_r", n))
-        push(x.at[own_rows(right), part], out.at[2 * c + k, own_rows(right), part], peer_of(right), ("c_left", n))
-        push(x.at[own_rows(left), part], out.at[2 * c + k, own_rows(left), part], peer_of(left), ("c_right", n))
+        push(x.at[rest_rows(right), part], out.at[2 * c + k, rest_rows(right), part], peer_of(right), ("c_left", n))
+        push(x.at[rest_rows(left), part], out.at[2 * c + k, rest_rows(left), part], peer_of(left), ("c_right", n))
+
+    def new_rows(mat, start, size, w_rows, get):
+        @pl.loop(0, size // STEP_ROWS)
+        def _(r):
+            w_part = w_rows(r)
+            part = ds(start + r * STEP_ROWS, STEP_ROWS)
+            ortho = get(part).astype(jnp.float32) * rms_scale
+            out[mat, part, :] = (w_part - LEARN_RATE * (ortho + WEIGHT_DECAY * w_part)).astype(jnp.bfloat16)
 
     def update(step, get):
         chip = order[step]
         arrived(w_buf.at[step % 2, ds(k * rows, rows)], ("w_own", step))
         arrived(w_buf.at[step % 2, ds((1 - k) * rows, rows)], ("w_sib", step))
-
-        @pl.loop(0, pair // STEP_ROWS)
-        def _(r):
-            w_part = w_buf[step % 2, ds(r * STEP_ROWS, STEP_ROWS), :]
-            part = ds(c * pair + r * STEP_ROWS, STEP_ROWS)
-            ortho = get(chip, part).astype(jnp.float32) * rms_scale
-            out[2 * chip + k, part, :] = (w_part - LEARN_RATE * (ortho + WEIGHT_DECAY * w_part)).astype(jnp.bfloat16)
-
+        start, size = (rest_start, rest) if step in (1, 2) else (0, pair)
+        new_rows(
+            2 * chip + k, c * pair + start, size, lambda r: w_buf[step % 2, ds(start + r * STEP_ROWS, STEP_ROWS), :],
+            lambda part: get(chip, part))
         if step + 2 < chips:
             load_w(step + 2)
-        push(mine(chip), mine(chip), peer_of(right), ("g_left", step))
-        push(mine(chip), mine(chip), peer_of(left), ("g_right", step))
-        push(mine(chip), mine(chip), sib, ("s_own", step))
+        place = out.at[2 * chip + k, block(c, step)]
+        push(place, place, peer_of(right), ("g_left", step))
+        push(place, place, peer_of(left), ("g_right", step))
+        push(place, place, sib, ("s_own", step))
+
+    def update_ahead():
+        for n, chip in enumerate((left, right)):
+            arrived(w_ahead.at[n], ("w_ahead_l", "w_ahead_r")[n])
+            new_rows(
+                2 * c + k, chip * pair + ahead_start, ahead, lambda r: w_ahead[n, ds(r * STEP_ROWS, STEP_ROWS), :],
+                lambda part: x[part, :])
+            place = out.at[2 * c + k, ahead_rows(chip)]
+            push(place, place, peer_of(right), ("e_left", n))
+            push(place, place, peer_of(left), ("e_right", n))
+            push(place, place, sib, ("s_ahead", n))
 
     update(0, lambda chip, part: x[part, :])
+    update_ahead()
     for n, part in enumerate(chunks):
         arrived(relay.at[0, :, part], ("c_relay_l", n))
         push(relay.at[0, :, part], out.at[2 * left + k, own_rows(right, 0), part], peer_of(right), ("c_opp_l", n))
@@ -280,54 +318,85 @@
     def returned(chip, part):
         return out[2 * chip + k, part, :]
 
-    def x_rows(chip, half, part):
-        return out.at[2 * chip + k, own_rows(c, half), part]
-
     for n, part in enumerate(chunks):
-        arrived(x_rows(left, None, part), ("c_left", n))
+        arrived(out.at[2 * left + k, rest_rows(c), part], ("c_left", n))
     update(1, returned)
     for n, part in enumerate(chunks):
-        arrived(x_rows(right, None, part), ("c_right", n))
+        arrived(out.at[2 * right + k, rest_rows(c), part], ("c_right", n))
     update(2, returned)
     for n, part in enumerate(chunks):
-        arrived(x_rows(opp, 0, part), ("c_opp_l", n))
-        arrived(x_rows(opp, 1, part), ("c_opp_r", n))
+        arrived(out.at[2 * opp + k, own_rows(c, 0), part], ("c_opp_l", n))
+        arrived(out.at[2 * opp + k, own_rows(c, 1), part], ("c_opp_r", n))
     update(3, returned)
 
     def near(chip, step):
         return lax.rem(chip + (0, chips - 1, 1, 2)[step], chips)
+
+    def pass_on(mat, part, peer, key):
+        push(out.at[mat, part], out.at[mat, part], peer, key)
 
     last = chips - 1
     for step in range(chips):
         mat_l, mat_r = 2 * near(left, step) + k, 2 * near(right, step) + k
-        whole_l, whole_r = out.at[mat_l, own_rows(left)], out.at[mat_r, own_rows(right)]
-        part_l, part_r = out.at[mat_l, own_rows(left, 0)], out.at[mat_r, own_rows(right, 1)]
-        arrived(whole_l, ("g_left", step))
+        arrived(out.at[mat_l, block(left, step)], ("g_left", step))
         if step < last:
-            push(part_l, part_l, peer_of(right), ("f_left", step))
+            pass_on(mat_l, block_part(left, step, 0), peer_of(right), ("f_left", step))
         else:
-            load(part_l, tail_r, "tail_r")
-        push(whole_l, whole_l, sib, ("s_left", step))
-        arrived(whole_r, ("g_right", step))
+            load(out.at[mat_l, block_part(left, step, 0)], tail_r, "tail_r")
+        pass_on(mat_l, block(left, step), sib, ("s_left", step))
+        arrived(out.at[mat_r, block(right, step)], ("g_right", step))
         if step < last:
-            push(part_r, part_r, peer_of(left), ("f_right", step))
+            pass_on(mat_r, block_part(right, step, 1), peer_of(left), ("f_right", step))
         else:
-            load(part_r, tail_l, "tail_l")
-        push(whole_r, whole_r, sib, ("s_right", step))
+            load(out.at[mat_r, block_part(right, step, 1)], tail_l, "tail_l")
+        pass_on(mat_r, block(right, step), sib, ("s_right", step))
+        if step == 0:
+            arrived(out.at[mat_l, ahead_rows(opp)], ("e_left", 0))
+            pass_on(mat_l, ahead_rows(opp), peer_of(right), "fe_left")
+            pass_on(mat_l, ahead_rows(opp), sib, ("s_ahead_l", 0))
+            arrived(out.at[mat_l, ahead_rows(c)], ("e_left", 1))
+            pass_on(mat_l, ahead_rows(c), sib, ("s_ahead_l", 1))
+            arrived(out.at[mat_r, ahead_rows(c)], ("e_right", 0))
+            pass_on(mat_r, ahead_rows(c), sib, ("s_ahead_r", 0))
+            arrived(out.at[mat_r, ahead_rows(opp)], ("e_right", 1))
+            pass_on(mat_r, ahead_rows(opp), peer_of(left), "fe_right")
+            pass_on(mat_r, ahead_rows(opp), sib, ("s_ahead_r", 1))
     for step in range(last):
         mat = 2 * near(opp, step) + k
-        part_l, part_r = out.at[mat, own_rows(opp, 0)], out.at[mat, own_rows(opp, 1)]
-        arrived(part_l, ("f_left", step))
-        push(part_l, part_l, sib, ("s_far_l", step))
-        arrived(part_r, ("f_right", step))
-        push(part_r, part_r, sib, ("s_far_r", step))
+        arrived(out.at[mat, block_part(opp, step, 0)], ("f_left", step))
+        pass_on(mat, block_part(opp, step, 0), sib, ("s_far_l", step))
+        arrived(out.at[mat, block_part(opp, step, 1)], ("f_right", step))
+        pass_on(mat, block_part(opp, step, 1), sib, ("s_far_r", step))
+        if step == 0:
+            arrived(out.at[mat, ahead_rows(right)], "fe_left")
+            pass_on(mat, ahead_rows(right), sib, "s_far_ahead_l")
+            arrived(out.at[mat, ahead_rows(left)], "fe_right")
+            pass_on(mat, ahead_rows(left), sib, "s_far_ahead_r")
+
+    def sib_ahead(chip):
+        return ds(chip * pair + (1 - k) * (pair - ahead), ahead)
+
+    def sib_start(chip, step):
+        return chip * pair + (k * ahead if step in (1, 2) else 0)
+
     for step in range(chips):
-        arrived(out.at[2 * near(c, step) + 1 - k, own_rows(c)], ("s_own", step))
-        arrived(out.at[2 * near(left, step) + 1 - k, own_rows(left)], ("s_left", step))
-        arrived(out.at[2 * near(right, step) + 1 - k, own_rows(right)], ("s_right", step))
+        size = sum(sizes[step])
+        arrived(out.at[2 * near(c, step) + 1 - k, ds(sib_start(c, step), size)], ("s_own", step))
+        arrived(out.at[2 * near(left, step) + 1 - k, ds(sib_start(left, step), size)], ("s_left", step))
+        arrived(out.at[2 * near(right, step) + 1 - k, ds(sib_start(right, step), size)], ("s_right", step))
         if step < last:
-            arrived(out.at[2 * near(opp, step) + 1 - k, own_rows(opp, 0)], ("s_far_l", step))
-            arrived(out.at[2 * near(opp, step) + 1 - k, own_rows(opp, 1)], ("s_far_r", step))
+            mat, start = 2 * near(opp, step) + 1 - k, sib_start(opp, step)
+            arrived(out.at[mat, ds(start, sizes[step][0])], ("s_far_l", step))
+            arrived(out.at[mat, ds(start + sizes[step][0], sizes[step][1])], ("s_far_r", step))
+        if step == 0:
+            for n, chip in enumerate((left, right)):
+                arrived(out.at[2 * c + 1 - k, sib_ahead(chip)], ("s_ahead", n))
+            for n, chip in enumerate((opp, c)):
+                arrived(out.at[2 * left + 1 - k, sib_ahead(chip)], ("s_ahead_l", n))
+            for n, chip in enumerate((c, opp)):
+                arrived(out.at[2 * right + 1 - k, sib_ahead(chip)], ("s_ahead_r", n))
+            arrived(out.at[2 * opp + 1 - k, sib_ahead(right)], "s_far_ahead_l")
+            arrived(out.at[2 * opp + 1 - k, sib_ahead(left)], "s_far_ahead_r")
     arrived(tail_r, "tail_r")
     arrived(tail_l, "tail_l")
     for copy in sent:
@@ -358,6 +427,7 @@
             pltpu.VMEM((dim, dim), jnp.bfloat16),
             pltpu.VMEM((2, rows, cols), jnp.bfloat16),
             pltpu.VMEM((2, pair, cols), jnp.float32),
+            pltpu.VMEM((2, rows // 2, cols), jnp.float32),
             pltpu.VMEM((2, group, 8, 128), jnp.float32),
             pltpu.SemaphoreType.DMA((128,)),
             pltpu.SemaphoreType.DMA((128,)),
@@ -365,7 +435,7 @@
             pltpu.SemaphoreType.REGULAR,
         ],
         compiler_params=pltpu.CompilerParams(
-            collective_id=0, has_side_effects=True, vmem_limit_bytes=15 * 1024 * 1024
+            collective_id=0, has_side_effects=True, vmem_limit_bytes=16 * 1024 * 1024
         ),
     )(mom, grad, w)
 

time: 289 us -> 283 us (0.979)
  Pallas kernels: 284 us -> 278 us
    pallas_call x1, Pallas kernels: 266 us -> 260 us  [muon_step(): pl.pallas_call(functools.partial(muon_kernel, group), in_specs=[hbm, hbm,...]
where the time goes in v5:
time: 283 us
  Pallas kernels  278 us (98%)
  starting transfers between devices  4.12 us (1%)
    pallas_call x1, Pallas kernels, muon_step(): pl.pallas_call(functools.partial(muon_kernel, group), in_specs=[hbm, hbm,...  260 us
    pallas_call x2, Pallas kernels, store_step(): pl.pallas_call(store_kernel, in_specs=[pl.BlockSpec(memory_space=pltpu.VM...  16 us
  transfers between devices with their start and end apart: 4, of which 1 were waited for; matrix products, arithmetic and copies ran while one was open for 0% of the time, Pallas kernels for 6%

profile of v5, /device:TPU:81, one launch (start us, length us, event | category | flops | bytes accessed | tf_op | source)
XLA Modules:
  0.0 283.2 jit_solution(8332025797157050133)
XLA Ops:
  0.6 259.9 %shard_map.50 = (bf16[8,768,3072]{2,1,0:T(8,128)(2,1)S(1)}, f32[8,96,3072]{2,1,0:T(8,128)S(1)}, f32[4,96,3072]{2,1,0:T(8,128)}, bf16[96,3072]{1,0:T(8,128)(2,1)}, bf16[96,3072]{1,0:T(8,128)(2,1)}) custom-call(f32[8,96,3072]{2,1,0:T(8,128)} %mom.1, bf16[8,96,3072]{2,1,0:T(8,128)(2,1)} %grad.1, f32[8,96,3072]{2,1,0:T(8,128)} %w.1), custom_call_target="tpu_custom_call" | custom-call | tf_op jit(solution)/shard_map/pallas_call | solution.py:413
  260.5 0.8 collective-permute-start
  261.3 1.9 collective-permute-start.1
  263.3 12.3 %shard_map.51.params = bf16[8,768,3072]{2,1,0:T(8,128)(2,1)} custom-call(bf16[8,768,3072]{2,1,0:T(8,128)(2,1)S(1)} %get-tuple-element.14.src), custom_call_target="tpu_custom_call" | custom-call | flops 18874368000 | bytes 37748736 | tf_op jit(solution)/shard_map/pallas_call | solution.py:452
  275.6 0.6 collective-permute-done.near_l
  276.2 0.0 collective-permute-done.1.near_r
  276.2 1.4 collective-permute-start.2
  277.6 0.0 collective-permute-start.3
  277.6 3.7 %shard_map.52 = f32[8,96,3072]{2,1,0:T(8,128)} custom-call(f32[8,96,3072]{2,1,0:T(8,128)S(1)} %get-tuple-element.18.src), custom_call_target="tpu_custom_call" | custom-call | flops 2359296000 | bytes 4718592 | tf_op jit(solution)/shard_map/pallas_call | solution.py:452
  281.3 0.0 collective-permute-done.2.far_l
  281.3 0.0 collective-permute-done.3.far_r
  281.3 1.9 shard_map.53
Async XLA Ops:
  260.5 15.7 %collective-permute-start = (bf16[96,3072]{1,0:T(8,128)(2,1)}, bf16[96,3072]{1,0:T(8,128)(2,1)S(1)}, u32[]{:S(2)}, u32[]{:S(2)}) collective-permute-start(bf16[96,3072]{1,0:T(8,128)(2,1)} %get-tuple-element.12), channel_id=1, source_target_pairs={{0,2},{1,3},{2,4},{3,5},{4,6},{5,7},{6,0},{7,1},{8,10},{9,11},{10,... | collective-permute-start | bytes 1769480 | tf_op jit(solution)/shard_map/ppermute | solution.py:508
  261.3 14.9 %collective-permute-start.1 = (bf16[96,3072]{1,0:T(8,128)(2,1)}, bf16[96,3072]{1,0:T(8,128)(2,1)S(1)}, u32[]{:S(2)}, u32[]{:S(2)}) collective-permute-start(bf16[96,3072]{1,0:T(8,128)(2,1)} %get-tuple-element.13), channel_id=1, source_target_pairs={{0,6},{1,7},{2,0},{3,1},{4,2},{5,3},{6,4},{7,5},{8,14},{9,15},{10,... | collective-permute-start | bytes 1769480 | tf_op jit(solution)/shard_map/ppermute | solution.py:508
  276.2 5.1 %collective-permute-start.2 = (bf16[96,3072]{1,0:T(8,128)(2,1)S(1)}, bf16[96,3072]{1,0:T(8,128)(2,1)S(1)}, u32[]{:S(2)}, u32[]{:S(2)}) collective-permute-start(bf16[96,3072]{1,0:T(8,128)(2,1)S(1)} %collective-permute-done.near_l), channel_id=1, source_target_pairs={{0,1},{1,0},{2,3},{3,2},{4,5},{5,4},{6,7},{7,6},{8,9},{9,8},{10,11... | collective-permute-start | bytes 1769480 | tf_op jit(solution)/shard_map/ppermute | solution.py:511
  277.6 3.7 %collective-permute-start.3 = (bf16[96,3072]{1,0:T(8,128)(2,1)S(1)}, bf16[96,3072]{1,0:T(8,128)(2,1)S(1)}, u32[]{:S(2)}, u32[]{:S(2)}) collective-permute-start(bf16[96,3072]{1,0:T(8,128)(2,1)S(1)} %collective-permute-done.1.near_r), channel_id=1, source_target_pairs={{0,1},{1,0},{2,3},{3,2},{4,5},{5,4},{6,7},{7,6},{8,9},{9,8},{10,11... | collective-permute-start | bytes 1769480 | tf_op jit(solution)/shard_map/ppermute | solution.py:511

commit v6 on v5

--- a/solution.py
+++ b/solution.py
@@ -22,6 +22,7 @@
 WIDE = 1024
 SCALE_ROWS = 32
 STEP_ROWS = 16
+PREFETCH = 3
 
 
 def ds(start, size):
@@ -125,11 +126,17 @@
     def arrived(dst, key):
         pltpu.make_async_copy(dst, dst, recv.at[slot(key)]).wait()
 
-    steps = (opp, right, left, c)
-    for step, chip in enumerate(steps):
-        for par in range(2):
+    steps = (opp, left, right, c)
+
+    def prefetch(n):
+        if n < mats:
+            par, step = divmod(n, chips)
+            chip = steps[step]
             load(mom.at[2 * chip + par], mom_new.at[2 * chip + par], ("mom", step, par))
             load(grad.at[2 * chip + par], out.at[2 * chip + k, own_rows(left, par)], ("grad", step, par))
+
+    for n in range(PREFETCH):
+        prefetch(n)
 
     barrier = pltpu.get_barrier_semaphore()
     for step in range(1, group):
@@ -141,6 +148,7 @@
         base = jnp.where(k == par, c * pair + k * rows, right * pair)
         arrived(mom_new.at[mat], ("mom", step, par))
         arrived(out.at[2 * chip + k, own_rows(left, par)], ("grad", step, par))
+        prefetch(par * chips + step + PREFETCH)
 
         def body(r, total):
             part = ds(r * STEP_ROWS, STEP_ROWS)
@@ -167,15 +175,13 @@
             remote(mine(opp, 0), relay.at[0], peer_of(right), "a_relay_l"),
             remote(mine(opp, 1), relay.at[1], peer_of(left), "a_relay_r"),
         ],
-        [remote(mine(right), x.at[own_rows(c)], peer_of(right), "a_left")],
-        [remote(mine(left), x.at[own_rows(c)], peer_of(left), "a_right")],
+        [remote(mine(left, half), x.at[own_rows(c, half)], peer_of(left), ("a_right", half)) for half in range(2)],
+        [remote(mine(right, half), x.at[own_rows(c, half)], peer_of(right), ("a_left", half)) for half in range(2)],
         [],
     ]
 
-    def send_rows(step, chip):
-        arrived(mine(chip, 1 - k), ("swap", step))
-        for copy in exchange[step]:
-            copy.start()
+    def swapped(step):
+        arrived(mine(steps[step], 1 - k), ("swap", step))
 
     for step, chip in enumerate(steps):
         momentum(step, chip, 0)
@@ -186,7 +192,12 @@
 
         @pl.when(k == 0)
         def _():
-            send_rows(step, chip)
+            for copy in exchange[step][:1]:
+                copy.start()
+            if step > 0:
+                swapped(step - 1)
+                for copy in exchange[step - 1][1:]:
+                    copy.start()
 
     for step, chip in enumerate(steps):
         momentum(step, chip, 1)
@@ -194,6 +205,8 @@
         @pl.when(k == 0)
         def _():
             swap[step].start()
+            if step == 0:
+                swapped(chips - 1)
 
     for step in range(1, group):
         dest = lax.rem(me + step, group)
@@ -204,8 +217,10 @@
     @pl.when(k == 1)
     def _():
         pl.semaphore_wait(go, 1)
-        for step, chip in enumerate(steps):
-            send_rows(step, chip)
+        for step in range(chips):
+            swapped(step)
+            for copy in exchange[step]:
+                copy.start()
 
     arrived(relay.at[0], "a_relay_l")
     pass_right = push(relay.at[0], x.at[own_rows(left, 0)], peer_of(right), "a_opp_l")
@@ -228,9 +243,11 @@
             x[part, :] = (get(part).astype(jnp.float32) * inverse).astype(jnp.bfloat16)
 
     scale(lambda part: out[2 * c + k, part, :], c * pair)
-    arrived(x.at[own_rows(left)], "a_left")
+    for half in range(2):
+        arrived(x.at[own_rows(left, half)], ("a_left", half))
     scale(lambda part: x[part, :], left * pair)
-    arrived(x.at[own_rows(right)], "a_right")
+    for half in range(2):
+        arrived(x.at[own_rows(right, half)], ("a_right", half))
     scale(lambda part: x[part, :], right * pair)
     arrived(x.at[own_rows(opp, 0)], "a_opp_l")
     arrived(x.at[own_rows(opp, 1)], "a_opp_r")
@@ -280,6 +297,8 @@
             part = ds(start + r * STEP_ROWS, STEP_ROWS)
             ortho = get(part).astype(jnp.float32) * rms_scale
             out[mat, part, :] = (w_part - LEARN_RATE * (ortho + WEIGHT_DECAY * w_part)).astype(jnp.bfloat16)
+
+    last = chips - 1
 
     def update(step, get):
         chip = order[step]
@@ -292,8 +311,14 @@
         if step + 2 < chips:
             load_w(step + 2)
         place = out.at[2 * chip + k, block(c, step)]
-        push(place, place, peer_of(right), ("g_left", step))
-        push(place, place, peer_of(left), ("g_right", step))
+        if step < last:
+            push(place, place, peer_of(right), ("g_left", step))
+            push(place, place, peer_of(left), ("g_right", step))
+        else:
+            parts = [out.at[2 * chip + k, block_part(c, step, way)] for way in range(2)]
+            for way in range(2):
+                push(parts[way], parts[way], peer_of(right), ("g_left", step, way))
+                push(parts[1 - way], parts[1 - way], peer_of(left), ("g_right", step, 1 - way))
         push(place, place, sib, ("s_own", step))
 
     def update_ahead():
@@ -335,20 +360,13 @@
     def pass_on(mat, part, peer, key):
         push(out.at[mat, part], out.at[mat, part], peer, key)
 
-    last = chips - 1
-    for step in range(chips):
+    for step in range(last):
         mat_l, mat_r = 2 * near(left, step) + k, 2 * near(right, step) + k
         arrived(out.at[mat_l, block(left, step)], ("g_left", step))
-        if step < last:
-            pass_on(mat_l, block_part(left, step, 0), peer_of(right), ("f_left", step))
-        else:
-            load(out.at[mat_l, block_part(left, step, 0)], tail_r, "tail_r")
+        pass_on(mat_l, block_part(left, step, 0), peer_of(right), ("f_left", step))
         pass_on(mat_l, block(left, step), sib, ("s_left", step))
         arrived(out.at[mat_r, block(right, step)], ("g_right", step))
-        if step < last:
-            pass_on(mat_r, block_part(right, step, 1), peer_of(left), ("f_right", step))
-        else:
-            load(out.at[mat_r, block_part(right, step, 1)], tail_l, "tail_l")
+        pass_on(mat_r, block_part(right, step, 1), peer_of(left), ("f_right", step))
         pass_on(mat_r, block(right, step), sib, ("s_right", step))
         if step == 0:
             arrived(out.at[mat_l, ahead_rows(opp)], ("e_left", 0))
@@ -361,6 +379,16 @@
             arrived(out.at[mat_r, ahead_rows(opp)], ("e_right", 1))
             pass_on(mat_r, ahead_rows(opp), peer_of(left), "fe_right")
             pass_on(mat_r, ahead_rows(opp), sib, ("s_ahead_r", 1))
+    mat_l, mat_r = 2 * near(left, last) + k, 2 * near(right, last) + k
+    for way in range(2):
+        arrived(out.at[mat_l, block_part(left, last, way)], ("g_left", last, way))
+        pass_on(mat_l, block_part(left, last, way), sib, ("s_left", last, way))
+        arrived(out.at[mat_r, block_part(right, last, 1 - way)], ("g_right", last, 1 - way))
+        pass_on(mat_r, block_part(right, last, 1 - way), sib, ("s_right", last, 1 - way))
+        if way == 0:
+            load(out.at[mat_l, block_part(left, last, 0)], tail_r, "tail_r")
+            load(out.at[mat_r, block_part(right, last, 1)], tail_l, "tail_l")
+
     for step in range(last):
         mat = 2 * near(opp, step) + k
         arrived(out.at[mat, block_part(opp, step, 0)], ("f_left", step))
@@ -382,9 +410,13 @@
     for step in range(chips):
         size = sum(sizes[step])
         arrived(out.at[2 * near(c, step) + 1 - k, ds(sib_start(c, step), size)], ("s_own", step))
-        arrived(out.at[2 * near(left, step) + 1 - k, ds(sib_start(left, step), size)], ("s_left", step))
-        arrived(out.at[2 * near(right, step) + 1 - k, ds(sib_start(right, step), size)], ("s_right", step))
-        if step < last:
+        if step == last:
+            for way in range(2):
+                arrived(out.at[2 * near(left, step) + 1 - k, own_rows(left, way)], ("s_left", step, way))
+                arrived(out.at[2 * near(right, step) + 1 - k, own_rows(right, way)], ("s_right", step, way))
+        else:
+            arrived(out.at[2 * near(left, step) + 1 - k, ds(sib_start(left, step), size)], ("s_left", step))
+            arrived(out.at[2 * near(right, step) + 1 - k, ds(sib_start(right, step), size)], ("s_right", step))
             mat, start = 2 * near(opp, step) + 1 - k, sib_start(opp, step)
             arrived(out.at[mat, ds(start, sizes[step][0])], ("s_far_l", step))
             arrived(out.at[mat, ds(start + sizes[step][0], sizes[step][1])], ("s_far_r", step))
@@ -440,57 +472,70 @@
     )(mom, grad, w)
 
 
-def store_kernel(src, dst, sem):
-    copies = [pltpu.make_async_copy(src.at[i], dst.at[i], sem.at[i]) for i in range(src.shape[0])]
+def run_copies(pairs, sem):
+    copies = [pltpu.make_async_copy(src, dst, sem.at[n]) for n, (src, dst) in enumerate(pairs)]
     for copy in copies:
         copy.start()
     for copy in copies:
         copy.wait()
 
 
-def store_step(full):
+def place_of(params, group):
+    me = lax.axis_index("data")
+    rows = params.shape[1] // group
+    chips = group // 2
+
+    def part(chip, half=None):
+        start = 2 * lax.rem(chip, chips) + (0 if half is None else half)
+        return ds(start * rows, 2 * rows if half is None else rows)
+
+    return lax.div(me, 2), lax.rem(me, 2), chips, part
+
+
+def store_params_kernel(group, src, dst, sem):
+    c, _, chips, part = place_of(src, group)
+    pairs = []
+    for par in range(2):
+        for step in range(1, chips):
+            mat = 2 * lax.rem(c + step, chips) + par
+            pairs.append((src.at[mat], dst.at[mat]))
+        for step in (0, 1, chips - 1):
+            where = (2 * c + par, part(c + step))
+            pairs.append((src.at[where], dst.at[where]))
+    run_copies(pairs, sem)
+
+
+def store_kernel(src, dst, sem):
+    run_copies([(src.at[i], dst.at[i]) for i in range(src.shape[0])], sem)
+
+
+def store_late_kernel(group, params, near_l, near_r, far_l, far_r, out, sem):
+    c, k, _, part = place_of(out, group)
+    pieces = ((near_l, k, 0), (near_r, k, 1), (far_l, 1 - k, 0), (far_r, 1 - k, 1))
+    run_copies([(src, out.at[2 * c + par, part(c + 2, half)]) for src, par, half in pieces], sem)
+
+
+def store_step(kernel, full, copies):
     return pl.pallas_call(
-        store_kernel,
+        kernel,
         in_specs=[pl.BlockSpec(memory_space=pltpu.VMEM)],
         out_specs=pl.BlockSpec(memory_space=pl.ANY),
         out_shape=jax.ShapeDtypeStruct(full.shape, full.dtype),
-        scratch_shapes=[pltpu.SemaphoreType.DMA((full.shape[0],))],
+        scratch_shapes=[pltpu.SemaphoreType.DMA((copies,))],
         compiler_params=pltpu.CompilerParams(vmem_limit_bytes=1024 * 1024),
         cost_estimate=pl.CostEstimate(flops=1000 * full.size, bytes_accessed=2 * full.size, transcendentals=0),
     )(full)
 
 
-def tail_kernel(params, near_l, near_r, far_l, far_r, out, buf, sem):
-    rows = buf.shape[1]
-    pair = 2 * rows
-    chips = params.shape[1] // pair
-    me = lax.axis_index("data")
-    c, k = lax.div(me, 2), lax.rem(me, 2)
-    start = lax.rem(c + 2, chips) * pair
-    pieces = ((near_l, k, 0), (near_r, k, 1), (far_l, 1 - k, 0), (far_r, 1 - k, 1))
-    loads = [pltpu.make_async_copy(src, buf.at[n], sem.at[n]) for n, (src, _, _) in enumerate(pieces)]
-    stores = [
-        pltpu.make_async_copy(buf.at[n], out.at[2 * c + par, pl.ds(pl.multiple_of(start + half * rows, rows), rows)], sem.at[n])
-        for n, (_, par, half) in enumerate(pieces)
-    ]
-    for copy in loads:
-        copy.start()
-    for copy, store in zip(loads, stores):
-        copy.wait()
-        store.start()
-    for store in stores:
-        store.wait()
-
-
-def tail_step(params, pieces):
+def store_late(group, params, pieces):
     hbm = pl.BlockSpec(memory_space=pl.ANY)
     return pl.pallas_call(
-        tail_kernel,
-        in_specs=[hbm] * 5,
+        functools.partial(store_late_kernel, group),
+        in_specs=[hbm] + [pl.BlockSpec(memory_space=pltpu.VMEM)] * 4,
         out_specs=hbm,
         out_shape=jax.ShapeDtypeStruct(params.shape, params.dtype),
         input_output_aliases={0: 0},
-        scratch_shapes=[pltpu.VMEM((4, *pieces[0].shape), pieces[0].dtype), pltpu.SemaphoreType.DMA((4,))],
+        scratch_shapes=[pltpu.SemaphoreType.DMA((4,))],
         compiler_params=pltpu.CompilerParams(vmem_limit_bytes=4 * 1024 * 1024),
     )(params, *pieces)
 
@@ -506,12 +551,12 @@
         to_left = [(d, (d - 2) % group) for d in range(group)]
         swap = [(d, d + 1 - 2 * (d % 2)) for d in range(group)]
         near = [lax.ppermute(tail_r, "data", to_right), lax.ppermute(tail_l, "data", to_left)]
-        params = store_step(params)
+        params = store_step(functools.partial(store_params_kernel, group), params, 2 * (group // 2 + 2))
         *near, params = lax.optimization_barrier((*near, params))
         far = [lax.ppermute(piece, "data", swap) for piece in near]
-        mom_new = store_step(mom_new)
+        mom_new = store_step(store_kernel, mom_new, mom_new.shape[0])
         *far, mom_new = lax.optimization_barrier((*far, mom_new))
-        return tail_step(params, near + far), mom_new
+        return store_late(group, params, near + far), mom_new
 
     return jax.shard_map(
         local_step, mesh=mesh, in_specs=(row_spec, row_spec, row_spec), out_specs=(full_spec, row_spec), check_vma=False

time: 283 us -> 281 us (level)
  Pallas kernels: 278 us -> 275 us
  transfers between devices with their start and end apart: 4 -> 4, of which waited for: 1 -> 1; matrix products, arithmetic and copies ran while one was open for 0% -> 0% of each run, Pallas kernels for 6% -> 5%
where the time goes in v6:
time: 281 us
  Pallas kernels  275 us (98%)
  starting transfers between devices  4.13 us (1%)
    pallas_call x1, Pallas kernels, muon_step(): pl.pallas_call(functools.partial(muon_kernel, group), in_specs=[hbm, hbm,...  258 us
    pallas_call x2, Pallas kernels, store_step(): pl.pallas_call(kernel, in_specs=[pl.BlockSpec(memory_space=pltpu.VMEM)],...  15.2 us
  transfers between devices with their start and end apart: 4, of which 1 were waited for; matrix products, arithmetic and copies ran while one was open for 0% of the time, Pallas kernels for 5%

profile of v6, /device:TPU:81, one launch (start us, length us, event | category | flops | bytes accessed | tf_op | source)
XLA Modules:
  0.0 281.3 jit_solution(8591027931141089728)
XLA Ops:
  0.6 258.4 %shard_map.50 = (bf16[8,768,3072]{2,1,0:T(8,128)(2,1)S(1)}, f32[8,96,3072]{2,1,0:T(8,128)S(1)}, f32[4,96,3072]{2,1,0:T(8,128)}, bf16[96,3072]{1,0:T(8,128)(2,1)}, bf16[96,3072]{1,0:T(8,128)(2,1)}) custom-call(f32[8,96,3072]{2,1,0:T(8,128)} %mom.1, bf16[8,96,3072]{2,1,0:T(8,128)(2,1)} %grad.1, f32[8,96,3072]{2,1,0:T(8,128)} %w.1), custom_call_target="tpu_custom_call" | custom-call | tf_op jit(solution)/shard_map/pallas_call | solution.py:445
  259.0 0.7 collective-permute-start
  259.7 2.1 collective-permute-start.1
  261.8 11.5 %shard_map.51.params = bf16[8,768,3072]{2,1,0:T(8,128)(2,1)} custom-call(bf16[8,768,3072]{2,1,0:T(8,128)(2,1)S(1)} %get-tuple-element.14.src), custom_call_target="tpu_custom_call" | custom-call | flops 18874368000 | bytes 37748736 | tf_op jit(solution)/shard_map/pallas_call | solution.py:519
  273.4 1.4 collective-permute-done.near_l
  274.7 0.0 collective-permute-done.1.near_r
  274.7 1.4 collective-permute-start.2
  276.1 0.0 collective-permute-start.3
  276.1 3.7 %shard_map.52 = f32[8,96,3072]{2,1,0:T(8,128)} custom-call(f32[8,96,3072]{2,1,0:T(8,128)S(1)} %get-tuple-element.18.src), custom_call_target="tpu_custom_call" | custom-call | flops 2359296000 | bytes 4718592 | tf_op jit(solution)/shard_map/pallas_call | solution.py:519
  279.8 0.0 collective-permute-done.2.far_l
  279.8 0.0 collective-permute-done.3.far_r
  279.8 1.5 shard_map.53
Async XLA Ops:
  259.0 15.7 %collective-permute-start = (bf16[96,3072]{1,0:T(8,128)(2,1)}, bf16[96,3072]{1,0:T(8,128)(2,1)S(1)}, u32[]{:S(2)}, u32[]{:S(2)}) collective-permute-start(bf16[96,3072]{1,0:T(8,128)(2,1)} %get-tuple-element.12), channel_id=1, source_target_pairs={{0,2},{1,3},{2,4},{3,5},{4,6},{5,7},{6,0},{7,1},{8,10},{9,11},{10,... | collective-permute-start | bytes 1769480 | tf_op jit(solution)/shard_map/ppermute | solution.py:553
  259.7 15.0 %collective-permute-start.1 = (bf16[96,3072]{1,0:T(8,128)(2,1)}, bf16[96,3072]{1,0:T(8,128)(2,1)S(1)}, u32[]{:S(2)}, u32[]{:S(2)}) collective-permute-start(bf16[96,3072]{1,0:T(8,128)(2,1)} %get-tuple-element.13), channel_id=1, source_target_pairs={{0,6},{1,7},{2,0},{3,1},{4,2},{5,3},{6,4},{7,5},{8,14},{9,15},{10,... | collective-permute-start | bytes 1769480 | tf_op jit(solution)/shard_map/ppermute | solution.py:553
  274.7 5.1 %collective-permute-start.2 = (bf16[96,3072]{1,0:T(8,128)(2,1)S(1)}, bf16[96,3072]{1,0:T(8,128)(2,1)S(1)}, u32[]{:S(2)}, u32[]{:S(2)}) collective-permute-start(bf16[96,3072]{1,0:T(8,128)(2,1)S(1)} %collective-permute-done.near_l), channel_id=1, source_target_pairs={{0,1},{1,0},{2,3},{3,2},{4,5},{5,4},{6,7},{7,6},{8,9},{9,8},{10,11... | collective-permute-start | bytes 1769480 | tf_op jit(solution)/shard_map/ppermute | solution.py:556
  276.1 3.7 %collective-permute-start.3 = (bf16[96,3072]{1,0:T(8,128)(2,1)S(1)}, bf16[96,3072]{1,0:T(8,128)(2,1)S(1)}, u32[]{:S(2)}, u32[]{:S(2)}) collective-permute-start(bf16[96,3072]{1,0:T(8,128)(2,1)S(1)} %collective-permute-done.1.near_r), channel_id=1, source_target_pairs={{0,1},{1,0},{2,3},{3,2},{4,5},{5,4},{6,7},{7,6},{8,9},{9,8},{10,11... | collective-permute-start | bytes 1769480 | tf_op jit(solution)/shard_map/ppermute | solution.py:556

commit v7 on v6

--- a/solution.py
+++ b/solution.py
@@ -19,7 +19,7 @@
 
 MESH = pl.DeviceIdType.MESH
 TILE = 256
-WIDE = 1024
+WIDE = 512
 SCALE_ROWS = 32
 STEP_ROWS = 16
 PREFETCH = 3
@@ -141,7 +141,6 @@
     barrier = pltpu.get_barrier_semaphore()
     for step in range(1, group):
         pl.semaphore_signal(barrier, inc=1, device_id={"data": lax.rem(me + step, group)}, device_id_type=MESH)
-    pl.semaphore_wait(barrier, group - 1)
 
     def momentum(step, chip, par):
         mat = 2 * chip + par
@@ -185,6 +184,8 @@
 
     for step, chip in enumerate(steps):
         momentum(step, chip, 0)
+        if step == 0:
+            pl.semaphore_wait(barrier, group - 1)
 
         @pl.when(k == 1)
         def _():
@@ -461,8 +462,8 @@
             pltpu.VMEM((2, pair, cols), jnp.float32),
             pltpu.VMEM((2, rows // 2, cols), jnp.float32),
             pltpu.VMEM((2, group, 8, 128), jnp.float32),
-            pltpu.SemaphoreType.DMA((128,)),
-            pltpu.SemaphoreType.DMA((128,)),
+            pltpu.SemaphoreType.DMA((160,)),
+            pltpu.SemaphoreType.DMA((160,)),
             pltpu.SemaphoreType.REGULAR,
             pltpu.SemaphoreType.REGULAR,
         ],
@@ -552,10 +553,9 @@
         swap = [(d, d + 1 - 2 * (d % 2)) for d in range(group)]
         near = [lax.ppermute(tail_r, "data", to_right), lax.ppermute(tail_l, "data", to_left)]
         params = store_step(functools.partial(store_params_kernel, group), params, 2 * (group // 2 + 2))
-        *near, params = lax.optimization_barrier((*near, params))
+        mom_new = store_step(store_kernel, mom_new, mom_new.shape[0])
+        *near, params, mom_new = lax.optimization_barrier((*near, params, mom_new))
         far = [lax.ppermute(piece, "data", swap) for piece in near]
-        mom_new = store_step(store_kernel, mom_new, mom_new.shape[0])
-        *far, mom_new = lax.optimization_barrier((*far, mom_new))
         return store_late(group, params, near + far), mom_new
 
     return jax.shard_map(

time: 281 us -> 283 us (level)
  transfers between devices with their start and end apart: 4 -> 4, of which waited for: 1 -> 2; matrix products, arithmetic and copies ran while one was open for 0% -> 0% of each run, Pallas kernels for 5% -> 5%
where the time goes in v7:
time: 283 us
  Pallas kernels  276 us (98%)
  starting transfers between devices  4.09 us (1%)
    pallas_call x1, Pallas kernels, muon_step(): pl.pallas_call(functools.partial(muon_kernel, group), in_specs=[hbm, hbm,...  259 us
    pallas_call x2, Pallas kernels, store_step(): pl.pallas_call(kernel, in_specs=[pl.BlockSpec(memory_space=pltpu.VMEM)],...  15.2 us
  transfers between devices with their start and end apart: 4, of which 2 were waited for; matrix products, arithmetic and copies ran while one was open for 0% of the time, Pallas kernels for 5%

profile of v7, /device:TPU:81, one launch (start us, length us, event | category | flops | bytes accessed | tf_op | source)
XLA Modules:
  0.0 282.9 jit_solution(9327244196335530604)
XLA Ops:
  0.6 259.0 %shard_map.50 = (bf16[8,768,3072]{2,1,0:T(8,128)(2,1)S(1)}, f32[8,96,3072]{2,1,0:T(8,128)S(1)}, f32[4,96,3072]{2,1,0:T(8,128)}, bf16[96,3072]{1,0:T(8,128)(2,1)}, bf16[96,3072]{1,0:T(8,128)(2,1)}) custom-call(f32[8,96,3072]{2,1,0:T(8,128)} %mom.1, bf16[8,96,3072]{2,1,0:T(8,128)(2,1)} %grad.1, f32[8,96,3072]{2,1,0:T(8,128)} %w.1), custom_call_target="tpu_custom_call" | custom-call | tf_op jit(solution)/shard_map/pallas_call | solution.py:446
  259.6 0.3 collective-permute-start
  260.0 2.4 collective-permute-start.1
  262.4 11.5 %shard_map.51.params = bf16[8,768,3072]{2,1,0:T(8,128)(2,1)} custom-call(bf16[8,768,3072]{2,1,0:T(8,128)(2,1)S(1)} %get-tuple-element.12.src), custom_call_target="tpu_custom_call" | custom-call | flops 18874368000 | bytes 37748736 | tf_op jit(solution)/shard_map/pallas_call | solution.py:520
  273.9 3.7 %shard_map.52 = f32[8,96,3072]{2,1,0:T(8,128)} custom-call(f32[8,96,3072]{2,1,0:T(8,128)S(1)} %get-tuple-element.13.src), custom_call_target="tpu_custom_call" | custom-call | flops 2359296000 | bytes 4718592 | tf_op jit(solution)/shard_map/pallas_call | solution.py:520
  277.6 0.0 collective-permute-done.near_l
  277.7 0.0 collective-permute-done.1.near_r
  277.7 1.2 collective-permute-start.2
  278.9 0.1 collective-permute-start.3
  279.0 1.5 collective-permute-done.2.far_l
  280.5 0.8 collective-permute-done.3.far_r
  281.3 1.4 shard_map.53
Async XLA Ops:
  259.6 18.0 %collective-permute-start = (bf16[96,3072]{1,0:T(8,128)(2,1)}, bf16[96,3072]{1,0:T(8,128)(2,1)S(1)}, u32[]{:S(2)}, u32[]{:S(2)}) collective-permute-start(bf16[96,3072]{1,0:T(8,128)(2,1)} %get-tuple-element.10), channel_id=1, source_target_pairs={{0,2},{1,3},{2,4},{3,5},{4,6},{5,7},{6,0},{7,1},{8,10},{9,11},{10,... | collective-permute-start | bytes 1769480 | tf_op jit(solution)/shard_map/ppermute | solution.py:554
  260.0 17.7 %collective-permute-start.1 = (bf16[96,3072]{1,0:T(8,128)(2,1)}, bf16[96,3072]{1,0:T(8,128)(2,1)S(1)}, u32[]{:S(2)}, u32[]{:S(2)}) collective-permute-start(bf16[96,3072]{1,0:T(8,128)(2,1)} %get-tuple-element.11), channel_id=1, source_target_pairs={{0,6},{1,7},{2,0},{3,1},{4,2},{5,3},{6,4},{7,5},{8,14},{9,15},{10,... | collective-permute-start | bytes 1769480 | tf_op jit(solution)/shard_map/ppermute | solution.py:554
  277.7 2.8 %collective-permute-start.2 = (bf16[96,3072]{1,0:T(8,128)(2,1)S(1)}, bf16[96,3072]{1,0:T(8,128)(2,1)S(1)}, u32[]{:S(2)}, u32[]{:S(2)}) collective-permute-start(bf16[96,3072]{1,0:T(8,128)(2,1)S(1)} %collective-permute-done.near_l), channel_id=1, source_target_pairs={{0,1},{1,0},{2,3},{3,2},{4,5},{5,4},{6,7},{7,6},{8,9},{9,8},{10,11... | collective-permute-start | bytes 1769480 | tf_op jit(solution)/shard_map/ppermute | solution.py:558
  278.9 2.5 collective-permute-start.3

commit v8 on v6

--- a/solution.py
+++ b/solution.py
@@ -29,31 +29,41 @@
     return pl.ds(pl.multiple_of(start, math.gcd(size, STEP_ROWS)), size)
 
 
-def symmetric(dst, product, finish, dim):
+def mirror(dst, block, start, cols):
+    for i in range(start, start + block.shape[0], TILE):
+        if not cols.start <= i < cols.stop:
+            dst[cols, i : i + TILE] = block[i - start : i - start + TILE].T
+
+
+def outer(x, rows, cols):
+    prod = lax.dot_general(x[rows, :], x[cols, :], (((1,), (1,)), ((), ())), preferred_element_type=jnp.float32)
+    return prod.astype(jnp.bfloat16)
+
+
+def gram_of(x, gram, start, stop):
+    for j in range(start, stop, TILE):
+        cols = slice(j, j + TILE)
+        block = outer(x, slice(j, stop), cols)
+        gram[j:stop, cols] = block
+        mirror(gram, block, j, cols)
+
+
+def gram_last(x, gram):
+    dim = gram.shape[0]
+    cols = slice(dim - TILE, dim)
+    block = outer(x, slice(0, dim), cols)
+    gram[:, cols] = block
+    mirror(gram, block, 0, cols)
+
+
+def newton_schulz_poly(gram, poly):
+    dim = gram.shape[0]
     for j in range(0, dim, TILE):
-        cols = slice(j, j + TILE)
-        block = finish(product(slice(j, dim), cols), slice(j, dim), cols)
-        dst[j:, cols] = block
-        for i in range(j + TILE, dim, TILE):
-            dst[cols, i : i + TILE] = block[i - j : i - j + TILE].T
-
-
-def newton_schulz_poly(x, gram, poly):
-    dim = gram.shape[0]
-
-    def outer(rows, cols):
-        return lax.dot_general(x[rows, :], x[cols, :], (((1,), (1,)), ((), ())), preferred_element_type=jnp.float32)
-
-    def square(rows, cols):
-        return jnp.dot(gram[rows, :], gram[:, cols], preferred_element_type=jnp.float32)
-
-    symmetric(gram, outer, lambda prod, rows, cols: prod.astype(jnp.bfloat16), dim)
-    symmetric(
-        poly,
-        square,
-        lambda prod, rows, cols: (COEF_B * gram[rows, cols].astype(jnp.float32) + COEF_C * prod).astype(jnp.bfloat16),
-        dim,
-    )
+        rows, cols = slice(j, dim), slice(j, j + TILE)
+        square = jnp.dot(gram[rows, :], gram[:, cols], preferred_element_type=jnp.float32)
+        block = (COEF_B * gram[rows, cols].astype(jnp.float32) + COEF_C * square).astype(jnp.bfloat16)
+        poly[rows, cols] = block
+        mirror(poly, block, j, cols)
 
 
 def newton_schulz_step(x, poly, part):
@@ -170,13 +180,16 @@
         remote(out.at[2 * chip + k, own_rows(right, 0)], out.at[2 * chip + 1 - k, own_rows(c, k)], sib, ("swap", step))
         for step, chip in enumerate(steps)
     ]
+    def x_rows(place, start=0, size=pair):
+        return ds(place * pair + start, size)
+
     exchange = [
         [
             remote(mine(opp, 0), relay.at[0], peer_of(right), "a_relay_l"),
             remote(mine(opp, 1), relay.at[1], peer_of(left), "a_relay_r"),
         ],
-        [remote(mine(left, half), x.at[own_rows(c, half)], peer_of(left), ("a_right", half)) for half in range(2)],
-        [remote(mine(right, half), x.at[own_rows(c, half)], peer_of(right), ("a_left", half)) for half in range(2)],
+        [remote(mine(left, half), x.at[x_rows(2, half * rows, rows)], peer_of(left), ("a_right", half)) for half in range(2)],
+        [remote(mine(right, half), x.at[x_rows(1, half * rows, rows)], peer_of(right), ("a_left", half)) for half in range(2)],
         [],
     ]
 
@@ -223,9 +236,9 @@
                 copy.start()
 
     arrived(relay.at[0], "a_relay_l")
-    pass_right = push(relay.at[0], x.at[own_rows(left, 0)], peer_of(right), "a_opp_l")
+    pass_right = push(relay.at[0], x.at[x_rows(3, 0, rows)], peer_of(right), "a_opp_l")
     arrived(relay.at[1], "a_relay_r")
-    pass_left = push(relay.at[1], x.at[own_rows(right, 1)], peer_of(left), "a_opp_r")
+    pass_left = push(relay.at[1], x.at[x_rows(3, rows, rows)], peer_of(left), "a_opp_r")
     push(w.at[2 * right + k, ds(k * ahead, ahead)], w_ahead.at[0], peer_of(right), "w_ahead_l")
     push(w.at[2 * left + k, ds(k * ahead, ahead)], w_ahead.at[1], peer_of(left), "w_ahead_r")
 
@@ -236,27 +249,29 @@
     norm = jnp.sqrt(jnp.sum(total, keepdims=True))
     inverse = 1.0 / (norm + NORM_EPS)
 
-    def scale(get, base):
+    def scale(place, get):
         @pl.loop(0, pair // SCALE_ROWS)
         def _(r):
-            part = ds(base + r * SCALE_ROWS, SCALE_ROWS)
-            x[part, :] = (get(part).astype(jnp.float32) * inverse).astype(jnp.bfloat16)
-
-    scale(lambda part: out[2 * c + k, part, :], c * pair)
-    for half in range(2):
-        arrived(x.at[own_rows(left, half)], ("a_left", half))
-    scale(lambda part: x[part, :], left * pair)
-    for half in range(2):
-        arrived(x.at[own_rows(right, half)], ("a_right", half))
-    scale(lambda part: x[part, :], right * pair)
-    arrived(x.at[own_rows(opp, 0)], "a_opp_l")
-    arrived(x.at[own_rows(opp, 1)], "a_opp_r")
+            part = x_rows(place, r * SCALE_ROWS, SCALE_ROWS)
+            x[part, :] = (get(r, part).astype(jnp.float32) * inverse).astype(jnp.bfloat16)
+
+    def arrived_row(_, part):
+        return x[part, :]
+
+    scale(0, lambda r, _: out[2 * c + k, ds(c * pair + r * SCALE_ROWS, SCALE_ROWS), :])
+    for place, key in ((1, "a_left"), (2, "a_right")):
+        for half in range(2):
+            arrived(x.at[x_rows(place, half * rows, rows)], (key, half))
+        scale(place, arrived_row)
+    gram_of(x, gram, 0, dim - TILE)
+    arrived(x.at[x_rows(3, 0, rows)], "a_opp_l")
+    arrived(x.at[x_rows(3, rows, rows)], "a_opp_r")
 
     @pl.when(k == 0)
     def _():
         pl.semaphore_signal(go, inc=1, device_id={"data": sib}, device_id_type=MESH)
 
-    scale(lambda part: x[part, :], opp * pair)
+    scale(3, arrived_row)
 
     waited = swap + sum(exchange, []) + [pass_right, pass_left]
     for copy in waited:
@@ -274,28 +289,31 @@
     load_w(0)
     load_w(1)
 
+    gram_last(x, gram)
+
     @pl.loop(0, NS_ITERS - 1)
     def _(_):
-        newton_schulz_poly(x, gram, poly)
+        newton_schulz_poly(gram, poly)
         newton_schulz_step(x, poly, pl.ds(0, cols))
-
-    newton_schulz_poly(x, gram, poly)
+        gram_of(x, gram, 0, dim)
+
+    newton_schulz_poly(gram, poly)
     pl.semaphore_wait(free, 2)
 
     chunks = [pl.ds(start, WIDE) for start in range(0, cols, WIDE)]
     for n, part in enumerate(chunks):
         newton_schulz_step(x, poly, part)
-        push(x.at[own_rows(opp, 0), part], relay.at[0, :, part], peer_of(right), ("c_relay_l", n))
-        push(x.at[own_rows(opp, 1), part], relay.at[1, :, part], peer_of(left), ("c_relay_r", n))
-        push(x.at[rest_rows(right), part], out.at[2 * c + k, rest_rows(right), part], peer_of(right), ("c_left", n))
-        push(x.at[rest_rows(left), part], out.at[2 * c + k, rest_rows(left), part], peer_of(left), ("c_right", n))
+        push(x.at[x_rows(3, 0, rows), part], relay.at[0, :, part], peer_of(right), ("c_relay_l", n))
+        push(x.at[x_rows(3, rows, rows), part], relay.at[1, :, part], peer_of(left), ("c_relay_r", n))
+        push(x.at[x_rows(2, rest_start, rest), part], out.at[2 * c + k, rest_rows(right), part], peer_of(right), ("c_left", n))
+        push(x.at[x_rows(1, rest_start, rest), part], out.at[2 * c + k, rest_rows(left), part], peer_of(left), ("c_right", n))
 
     def new_rows(mat, start, size, w_rows, get):
         @pl.loop(0, size // STEP_ROWS)
         def _(r):
             w_part = w_rows(r)
             part = ds(start + r * STEP_ROWS, STEP_ROWS)
-            ortho = get(part).astype(jnp.float32) * rms_scale
+            ortho = get(r, part).astype(jnp.float32) * rms_scale
             out[mat, part, :] = (w_part - LEARN_RATE * (ortho + WEIGHT_DECAY * w_part)).astype(jnp.bfloat16)
 
     last = chips - 1
@@ -307,7 +325,7 @@
         start, size = (rest_start, rest) if step in (1, 2) else (0, pair)
         new_rows(
             2 * chip + k, c * pair + start, size, lambda r: w_buf[step % 2, ds(start + r * STEP_ROWS, STEP_ROWS), :],
-            lambda part: get(chip, part))
+            get)
         if step + 2 < chips:
             load_w(step + 2)
         place = out.at[2 * chip + k, block(c, step)]
@@ -326,13 +344,13 @@
             arrived(w_ahead.at[n], ("w_ahead_l", "w_ahead_r")[n])
             new_rows(
                 2 * c + k, chip * pair + ahead_start, ahead, lambda r: w_ahead[n, ds(r * STEP_ROWS, STEP_ROWS), :],
-                lambda part: x[part, :])
+                lambda r, _: x[x_rows(1 + n, ahead_start + r * STEP_ROWS, STEP_ROWS), :])
             place = out.at[2 * c + k, ahead_rows(chip)]
             push(place, place, peer_of(right), ("e_left", n))
             push(place, place, peer_of(left), ("e_right", n))
             push(place, place, sib, ("s_ahead", n))
 
-    update(0, lambda chip, part: x[part, :])
+    update(0, lambda r, _: x[x_rows(0, r * STEP_ROWS, STEP_ROWS), :])
     update_ahead()
     for n, part in enumerate(chunks):
         arrived(relay.at[0, :, part], ("c_relay_l", n))
@@ -340,19 +358,16 @@
         arrived(relay.at[1, :, part], ("c_relay_r", n))
         push(relay.at[1, :, part], out.at[2 * right + k, own_rows(left, 1), part], peer_of(left), ("c_opp_r", n))
 
-    def returned(chip, part):
-        return out[2 * chip + k, part, :]
-
     for n, part in enumerate(chunks):
         arrived(out.at[2 * left + k, rest_rows(c), part], ("c_left", n))
-    update(1, returned)
+    update(1, lambda _, part: out[2 * left + k, part, :])
     for n, part in enumerate(chunks):
         arrived(out.at[2 * right + k, rest_rows(c), part], ("c_right", n))
-    update(2, returned)
+    update(2, lambda _, part: out[2 * right + k, part, :])
     for n, part in enumerate(chunks):
         arrived(out.at[2 * opp + k, own_rows(c, 0), part], ("c_opp_l", n))
         arrived(out.at[2 * opp + k, own_rows(c, 1), part], ("c_opp_r", n))
-    update(3, returned)
+    update(3, lambda _, part: out[2 * opp + k, part, :])
 
     def near(chip, step):
         return lax.rem(chip + (0, chips - 1, 1, 2)[step], chips)
@@ -467,7 +482,7 @@
             pltpu.SemaphoreType.REGULAR,
         ],
         compiler_params=pltpu.CompilerParams(
-            collective_id=0, has_side_effects=True, vmem_limit_bytes=16 * 1024 * 1024
+            collective_id=0, has_side_effects=True, vmem_limit_bytes=18 * 1024 * 1024
         ),
     )(mom, grad, w)
 

time: 281 us -> 282 us (level)
  no operation moved by 1% of the time
where the time goes in v8:
time: 282 us; the launch traced here: 281 us
  Pallas kernels  275 us (98%)
  starting transfers between devices  4.13 us (1%)
    pallas_call x1, Pallas kernels, muon_step(): pl.pallas_call(functools.partial(muon_kernel, group), in_specs=[hbm, hbm,...  258 us
    pallas_call x2, Pallas kernels, store_step(): pl.pallas_call(kernel, in_specs=[pl.BlockSpec(memory_space=pltpu.VMEM)],...  15.2 us
  transfers between devices with their start and end apart: 4, of which 1 were waited for; matrix products, arithmetic and copies ran while one was open for 0% of the time, Pallas kernels for 5%

profile of v8, /device:TPU:81, one launch (start us, length us, event | category | flops | bytes accessed | tf_op | source)
XLA Modules:
  0.0 281.4 jit_solution(9262427586582017367)
XLA Ops:
  0.6 258.4 %shard_map.50 = (bf16[8,768,3072]{2,1,0:T(8,128)(2,1)S(1)}, f32[8,96,3072]{2,1,0:T(8,128)S(1)}, f32[4,96,3072]{2,1,0:T(8,128)}, bf16[96,3072]{1,0:T(8,128)(2,1)}, bf16[96,3072]{1,0:T(8,128)(2,1)}) custom-call(f32[8,96,3072]{2,1,0:T(8,128)} %mom.1, bf16[8,96,3072]{2,1,0:T(8,128)(2,1)} %grad.1, f32[8,96,3072]{2,1,0:T(8,128)} %w.1), custom_call_target="tpu_custom_call" | custom-call | tf_op jit(solution)/shard_map/pallas_call | solution.py:460
  259.0 0.7 collective-permute-start
  259.7 2.1 collective-permute-start.1
  261.8 11.5 %shard_map.51.params = bf16[8,768,3072]{2,1,0:T(8,128)(2,1)} custom-call(bf16[8,768,3072]{2,1,0:T(8,128)(2,1)S(1)} %get-tuple-element.14.src), custom_call_target="tpu_custom_call" | custom-call | flops 18874368000 | bytes 37748736 | tf_op jit(solution)/shard_map/pallas_call | solution.py:534
  273.4 1.4 collective-permute-done.near_l
  274.7 0.0 collective-permute-done.1.near_r
  274.7 1.4 collective-permute-start.2
  276.1 0.0 collective-permute-start.3
  276.1 3.7 %shard_map.52 = f32[8,96,3072]{2,1,0:T(8,128)} custom-call(f32[8,96,3072]{2,1,0:T(8,128)S(1)} %get-tuple-element.18.src), custom_call_target="tpu_custom_call" | custom-call | flops 2359296000 | bytes 4718592 | tf_op jit(solution)/shard_map/pallas_call | solution.py:534
  279.8 0.0 collective-permute-done.2.far_l
  279.8 0.0 collective-permute-done.3.far_r
  279.8 1.5 shard_map.53
Async XLA Ops:
  259.0 15.7 %collective-permute-start = (bf16[96,3072]{1,0:T(8,128)(2,1)}, bf16[96,3072]{1,0:T(8,128)(2,1)S(1)}, u32[]{:S(2)}, u32[]{:S(2)}) collective-permute-start(bf16[96,3072]{1,0:T(8,128)(2,1)} %get-tuple-element.12), channel_id=1, source_target_pairs={{0,2},{1,3},{2,4},{3,5},{4,6},{5,7},{6,0},{7,1},{8,10},{9,11},{10,... | collective-permute-start | bytes 1769480 | tf_op jit(solution)/shard_map/ppermute | solution.py:568
  259.7 15.0 %collective-permute-start.1 = (bf16[96,3072]{1,0:T(8,128)(2,1)}, bf16[96,3072]{1,0:T(8,128)(2,1)S(1)}, u32[]{:S(2)}, u32[]{:S(2)}) collective-permute-start(bf16[96,3072]{1,0:T(8,128)(2,1)} %get-tuple-element.13), channel_id=1, source_target_pairs={{0,6},{1,7},{2,0},{3,1},{4,2},{5,3},{6,4},{7,5},{8,14},{9,15},{10,... | collective-permute-start | bytes 1769480 | tf_op jit(solution)/shard_map/ppermute | solution.py:568
  274.7 5.1 %collective-permute-start.2 = (bf16[96,3072]{1,0:T(8,128)(2,1)S(1)}, bf16[96,3072]{1,0:T(8,128)(2,1)S(1)}, u32[]{:S(2)}, u32[]{:S(2)}) collective-permute-start(bf16[96,3072]{1,0:T(8,128)(2,1)S(1)} %collective-permute-done.near_l), channel_id=1, source_target_pairs={{0,1},{1,0},{2,3},{3,2},{4,5},{5,4},{6,7},{7,6},{8,9},{9,8},{10,11... | collective-permute-start | bytes 1769480 | tf_op jit(solution)/shard_map/ppermute | solution.py:571
  276.1 3.7 %collective-permute-start.3 = (bf16[96,3072]{1,0:T(8,128)(2,1)S(1)}, bf16[96,3072]{1,0:T(8,128)(2,1)S(1)}, u32[]{:S(2)}, u32[]{:S(2)}) collective-permute-start(bf16[96,3072]{1,0:T(8,128)(2,1)S(1)} %collective-permute-done.1.near_r), channel_id=1, source_target_pairs={{0,1},{1,0},{2,3},{3,2},{4,5},{5,4},{6,7},{7,6},{8,9},{9,8},{10,11... | collective-permute-start | bytes 1769480 | tf_op jit(solution)/shard_map/ppermute | solution.py:571

commit v9 on v8

--- a/solution.py
+++ b/solution.py
@@ -23,6 +23,7 @@
 SCALE_ROWS = 32
 STEP_ROWS = 16
 PREFETCH = 3
+AHEAD = 3
 
 
 def ds(start, size):
@@ -91,7 +92,7 @@
             return ds(chip * pair, pair)
         return ds(chip * pair + half * rows, rows)
 
-    ahead = rows // 2
+    ahead = rows // AHEAD
     ahead_start, rest_start, rest = k * (pair - ahead), (1 - k) * ahead, pair - ahead
 
     def ahead_rows(chip):
@@ -239,8 +240,8 @@
     pass_right = push(relay.at[0], x.at[x_rows(3, 0, rows)], peer_of(right), "a_opp_l")
     arrived(relay.at[1], "a_relay_r")
     pass_left = push(relay.at[1], x.at[x_rows(3, rows, rows)], peer_of(left), "a_opp_r")
-    push(w.at[2 * right + k, ds(k * ahead, ahead)], w_ahead.at[0], peer_of(right), "w_ahead_l")
-    push(w.at[2 * left + k, ds(k * ahead, ahead)], w_ahead.at[1], peer_of(left), "w_ahead_r")
+    push(w.at[2 * right + k, ds(k * (rows - ahead), ahead)], w_ahead.at[0], peer_of(right), "w_ahead_l")
+    push(w.at[2 * left + k, ds(k * (rows - ahead), ahead)], w_ahead.at[1], peer_of(left), "w_ahead_r")
 
     total = sq[0, me]
     for step in range(1, group):
@@ -474,7 +475,7 @@
             pltpu.VMEM((dim, dim), jnp.bfloat16),
             pltpu.VMEM((2, rows, cols), jnp.bfloat16),
             pltpu.VMEM((2, pair, cols), jnp.float32),
-            pltpu.VMEM((2, rows // 2, cols), jnp.float32),
+            pltpu.VMEM((2, rows // AHEAD, cols), jnp.float32),
             pltpu.VMEM((2, group, 8, 128), jnp.float32),
             pltpu.SemaphoreType.DMA((128,)),
             pltpu.SemaphoreType.DMA((128,)),

time: 282 us -> 283 us (level)
  no operation moved by 1% of the time
where the time goes in v9:
time: 283 us
  Pallas kernels  276 us (98%)
  starting transfers between devices  4.13 us (1%)
    pallas_call x1, Pallas kernels, muon_step(): pl.pallas_call(functools.partial(muon_kernel, group), in_specs=[hbm, hbm,...  260 us
    pallas_call x2, Pallas kernels, store_step(): pl.pallas_call(kernel, in_specs=[pl.BlockSpec(memory_space=pltpu.VMEM)],...  15.2 us
  transfers between devices with their start and end apart: 4, of which 1 were waited for; matrix products, arithmetic and copies ran while one was open for 0% of the time, Pallas kernels for 5%

profile of v9, /device:TPU:81, one launch (start us, length us, event | category | flops | bytes accessed | tf_op | source)
XLA Modules:
  0.0 282.6 jit_solution(12753710244214866560)
XLA Ops:
  0.6 259.6 %shard_map.50 = (bf16[8,768,3072]{2,1,0:T(8,128)(2,1)S(1)}, f32[8,96,3072]{2,1,0:T(8,128)S(1)}, f32[4,96,3072]{2,1,0:T(8,128)}, bf16[96,3072]{1,0:T(8,128)(2,1)}, bf16[96,3072]{1,0:T(8,128)(2,1)}) custom-call(f32[8,96,3072]{2,1,0:T(8,128)} %mom.1, bf16[8,96,3072]{2,1,0:T(8,128)(2,1)} %grad.1, f32[8,96,3072]{2,1,0:T(8,128)} %w.1), custom_call_target="tpu_custom_call" | custom-call | tf_op jit(solution)/shard_map/pallas_call | solution.py:461
  260.2 0.1 collective-permute-start
  260.4 2.7 collective-permute-start.1
  263.0 11.5 %shard_map.51.params = bf16[8,768,3072]{2,1,0:T(8,128)(2,1)} custom-call(bf16[8,768,3072]{2,1,0:T(8,128)(2,1)S(1)} %get-tuple-element.14.src), custom_call_target="tpu_custom_call" | custom-call | flops 18874368000 | bytes 37748736 | tf_op jit(solution)/shard_map/pallas_call | solution.py:535
  274.6 1.4 collective-permute-done.near_l
  275.9 0.0 collective-permute-done.1.near_r
  275.9 1.4 collective-permute-start.2
  277.3 0.0 collective-permute-start.3
  277.3 3.7 %shard_map.52 = f32[8,96,3072]{2,1,0:T(8,128)} custom-call(f32[8,96,3072]{2,1,0:T(8,128)S(1)} %get-tuple-element.18.src), custom_call_target="tpu_custom_call" | custom-call | flops 2359296000 | bytes 4718592 | tf_op jit(solution)/shard_map/pallas_call | solution.py:535
  281.0 0.0 collective-permute-done.2.far_l
  281.0 0.0 collective-permute-done.3.far_r
  281.0 1.5 shard_map.53
Async XLA Ops:
  260.2 15.7 %collective-permute-start = (bf16[96,3072]{1,0:T(8,128)(2,1)}, bf16[96,3072]{1,0:T(8,128)(2,1)S(1)}, u32[]{:S(2)}, u32[]{:S(2)}) collective-permute-start(bf16[96,3072]{1,0:T(8,128)(2,1)} %get-tuple-element.12), channel_id=1, source_target_pairs={{0,2},{1,3},{2,4},{3,5},{4,6},{5,7},{6,0},{7,1},{8,10},{9,11},{10,... | collective-permute-start | bytes 1769480 | tf_op jit(solution)/shard_map/ppermute | solution.py:569
  260.4 15.6 %collective-permute-start.1 = (bf16[96,3072]{1,0:T(8,128)(2,1)}, bf16[96,3072]{1,0:T(8,128)(2,1)S(1)}, u32[]{:S(2)}, u32[]{:S(2)}) collective-permute-start(bf16[96,3072]{1,0:T(8,128)(2,1)} %get-tuple-element.13), channel_id=1, source_target_pairs={{0,6},{1,7},{2,0},{3,1},{4,2},{5,3},{6,4},{7,5},{8,14},{9,15},{10,... | collective-permute-start | bytes 1769480 | tf_op jit(solution)/shard_map/ppermute | solution.py:569
  275.9 5.1 %collective-permute-start.2 = (bf16[96,3072]{1,0:T(8,128)(2,1)S(1)}, bf16[96,3072]{1,0:T(8,128)(2,1)S(1)}, u32[]{:S(2)}, u32[]{:S(2)}) collective-permute-start(bf16[96,3072]{1,0:T(8,128)(2,1)S(1)} %collective-permute-done.near_l), channel_id=1, source_target_pairs={{0,1},{1,0},{2,3},{3,2},{4,5},{5,4},{6,7},{7,6},{8,9},{9,8},{10,11... | collective-permute-start | bytes 1769480 | tf_op jit(solution)/shard_map/ppermute | solution.py:572
  277.3 3.7 %collective-permute-start.3 = (bf16[96,3072]{1,0:T(8,128)(2,1)S(1)}, bf16[96,3072]{1,0:T(8,128)(2,1)S(1)}, u32[]{:S(2)}, u32[]{:S(2)}) collective-permute-start(bf16[96,3072]{1,0:T(8,128)(2,1)S(1)} %collective-permute-done.1.near_r), channel_id=1, source_target_pairs={{0,1},{1,0},{2,3},{3,2},{4,5},{5,4},{6,7},{7,6},{8,9},{9,8},{10,11... | collective-permute-start | bytes 1769480 | tf_op jit(solution)/shard_map/ppermute | solution.py:572

commit v10 on v6

--- a/solution.py
+++ b/solution.py
@@ -141,7 +141,6 @@
     barrier = pltpu.get_barrier_semaphore()
     for step in range(1, group):
         pl.semaphore_signal(barrier, inc=1, device_id={"data": lax.rem(me + step, group)}, device_id_type=MESH)
-    pl.semaphore_wait(barrier, group - 1)
 
     def momentum(step, chip, par):
         mat = 2 * chip + par
@@ -185,6 +184,8 @@
 
     for step, chip in enumerate(steps):
         momentum(step, chip, 0)
+        if step == 0:
+            pl.semaphore_wait(barrier, group - 1)
 
         @pl.when(k == 1)
         def _():
@@ -505,8 +506,12 @@
     run_copies(pairs, sem)
 
 
-def store_kernel(src, dst, sem):
-    run_copies([(src.at[i], dst.at[i]) for i in range(src.shape[0])], sem)
+def store_first_kernel(count, src, dst, sem):
+    run_copies([(src.at[i], dst.at[i]) for i in range(count)], sem)
+
+
+def store_rest_kernel(count, src, _, dst, sem):
+    run_copies([(src.at[i], dst.at[i]) for i in range(count, src.shape[0])], sem)
 
 
 def store_late_kernel(group, params, near_l, near_r, far_l, far_r, out, sem):
@@ -525,6 +530,20 @@
         compiler_params=pltpu.CompilerParams(vmem_limit_bytes=1024 * 1024),
         cost_estimate=pl.CostEstimate(flops=1000 * full.size, bytes_accessed=2 * full.size, transcendentals=0),
     )(full)
+
+
+def store_rest(count, full, stored):
+    hbm = pl.BlockSpec(memory_space=pl.ANY)
+    return pl.pallas_call(
+        functools.partial(store_rest_kernel, count),
+        in_specs=[pl.BlockSpec(memory_space=pltpu.VMEM), hbm],
+        out_specs=hbm,
+        out_shape=jax.ShapeDtypeStruct(full.shape, full.dtype),
+        input_output_aliases={1: 0},
+        scratch_shapes=[pltpu.SemaphoreType.DMA((full.shape[0] - count,))],
+        compiler_params=pltpu.CompilerParams(vmem_limit_bytes=1024 * 1024),
+        cost_estimate=pl.CostEstimate(flops=1000 * full.size, bytes_accessed=2 * full.size, transcendentals=0),
+    )(full, stored)
 
 
 def store_late(group, params, pieces):
@@ -552,11 +571,13 @@
         swap = [(d, d + 1 - 2 * (d % 2)) for d in range(group)]
         near = [lax.ppermute(tail_r, "data", to_right), lax.ppermute(tail_l, "data", to_left)]
         params = store_step(functools.partial(store_params_kernel, group), params, 2 * (group // 2 + 2))
-        *near, params = lax.optimization_barrier((*near, params))
+        first = mom_new.shape[0] // 4
+        mom_out = store_step(functools.partial(store_first_kernel, first), mom_new, first)
+        *near, params, mom_out = lax.optimization_barrier((*near, params, mom_out))
         far = [lax.ppermute(piece, "data", swap) for piece in near]
-        mom_new = store_step(store_kernel, mom_new, mom_new.shape[0])
-        *far, mom_new = lax.optimization_barrier((*far, mom_new))
-        return store_late(group, params, near + far), mom_new
+        mom_out = store_rest(first, mom_new, mom_out)
+        *far, mom_out = lax.optimization_barrier((*far, mom_out))
+        return store_late(group, params, near + far), mom_out
 
     return jax.shard_map(
         local_step, mesh=mesh, in_specs=(row_spec, row_spec, row_spec), out_specs=(full_spec, row_spec), check_vma=False

time: 281 us -> 281 us (level)
    pallas_call x0 -> x1, Pallas kernels: none -> 2.97 us  [store_rest(): pl.pallas_call(functools.partial(store_rest_kernel, count), in_specs=[pl....]
  transfers between devices with their start and end apart: 4 -> 4, of which waited for: 1 -> 0; matrix products, arithmetic and copies ran while one was open for 0% -> 0% of each run, Pallas kernels for 5% -> 6%
where the time goes in v10:
time: 281 us
  Pallas kernels  276 us (98%)
  starting transfers between devices  4.09 us (1%)
    pallas_call x1, Pallas kernels, muon_step(): pl.pallas_call(functools.partial(muon_kernel, group), in_specs=[hbm, hbm,...  258 us
    pallas_call x2, Pallas kernels, store_step(): pl.pallas_call(kernel, in_specs=[pl.BlockSpec(memory_space=pltpu.VMEM)],...  13 us
  transfers between devices with their start and end apart: 4, of which 0 were waited for; matrix products, arithmetic and copies ran while one was open for 0% of the time, Pallas kernels for 6%

profile of v10, /device:TPU:81, one launch (start us, length us, event | category | flops | bytes accessed | tf_op | source)
XLA Modules:
  0.0 280.6 jit_solution(4493227382157931232)
XLA Ops:
  0.6 258.4 %shard_map.50 = (bf16[8,768,3072]{2,1,0:T(8,128)(2,1)S(1)}, f32[8,96,3072]{2,1,0:T(8,128)S(1)}, f32[4,96,3072]{2,1,0:T(8,128)}, bf16[96,3072]{1,0:T(8,128)(2,1)}, bf16[96,3072]{1,0:T(8,128)(2,1)}) custom-call(f32[8,96,3072]{2,1,0:T(8,128)} %mom.1, bf16[8,96,3072]{2,1,0:T(8,128)(2,1)} %grad.1, f32[8,96,3072]{2,1,0:T(8,128)} %w.1), custom_call_target="tpu_custom_call" | custom-call | tf_op jit(solution)/shard_map/pallas_call | solution.py:446
  259.0 0.3 collective-permute-start
  259.4 2.4 collective-permute-start.1
  261.8 11.5 %shard_map.51.params = bf16[8,768,3072]{2,1,0:T(8,128)(2,1)} custom-call(bf16[8,768,3072]{2,1,0:T(8,128)(2,1)S(1)} %get-tuple-element.15.src), custom_call_target="tpu_custom_call" | custom-call | flops 18874368000 | bytes 37748736 | tf_op jit(solution)/shard_map/pallas_call | solution.py:524
  273.4 1.4 shard_map.52._
  274.8 0.0 collective-permute-done.near_l
  274.8 0.0 collective-permute-done.1.near_r
  274.8 1.3 collective-permute-start.2
  276.1 0.0 collective-permute-start.3
  276.1 3.0 %shard_map.53 = f32[8,96,3072]{2,1,0:T(8,128)} custom-call(f32[8,96,3072]{2,1,0:T(8,128)S(1)} %get-tuple-element.16.src, f32[8,96,3072]{2,1,0:T(8,128)} %shard_map.52._), custom_call_target="tpu_custom_call", output_to_operand_aliasing={{}: (1, {})} | custom-call | flops 2359296000 | bytes 4718592 | tf_op jit(solution)/shard_map/pallas_call | solution.py:537
  279.1 0.0 collective-permute-done.2.far_l
  279.1 0.0 collective-permute-done.3.far_r
  279.1 1.5 shard_map.54
Async XLA Ops:
  259.0 15.7 %collective-permute-start = (bf16[96,3072]{1,0:T(8,128)(2,1)}, bf16[96,3072]{1,0:T(8,128)(2,1)S(1)}, u32[]{:S(2)}, u32[]{:S(2)}) collective-permute-start(bf16[96,3072]{1,0:T(8,128)(2,1)} %get-tuple-element.13), channel_id=1, source_target_pairs={{0,2},{1,3},{2,4},{3,5},{4,6},{5,7},{6,0},{7,1},{8,10},{9,11},{10,... | collective-permute-start | bytes 1769480 | tf_op jit(solution)/shard_map/ppermute | solution.py:572
  259.4 15.4 %collective-permute-start.1 = (bf16[96,3072]{1,0:T(8,128)(2,1)}, bf16[96,3072]{1,0:T(8,128)(2,1)S(1)}, u32[]{:S(2)}, u32[]{:S(2)}) collective-permute-start(bf16[96,3072]{1,0:T(8,128)(2,1)} %get-tuple-element.14), channel_id=1, source_target_pairs={{0,6},{1,7},{2,0},{3,1},{4,2},{5,3},{6,4},{7,5},{8,14},{9,15},{10,... | collective-permute-start | bytes 1769480 | tf_op jit(solution)/shard_map/ppermute | solution.py:572
  274.8 4.3 %collective-permute-start.2 = (bf16[96,3072]{1,0:T(8,128)(2,1)S(1)}, bf16[96,3072]{1,0:T(8,128)(2,1)S(1)}, u32[]{:S(2)}, u32[]{:S(2)}) collective-permute-start(bf16[96,3072]{1,0:T(8,128)(2,1)S(1)} %collective-permute-done.near_l), channel_id=1, source_target_pairs={{0,1},{1,0},{2,3},{3,2},{4,5},{5,4},{6,7},{7,6},{8,9},{9,8},{10,11... | collective-permute-start | bytes 1769480 | tf_op jit(solution)/shard_map/ppermute | solution.py:577
  276.1 3.0 %collective-permute-start.3 = (bf16[96,3072]{1,0:T(8,128)(2,1)S(1)}, bf16[96,3072]{1,0:T(8,128)(2,1)S(1)}, u32[]{:S(2)}, u32[]{:S(2)}) collective-permute-start(bf16[96,3072]{1,0:T(8,128)(2,1)S(1)} %collective-permute-done.1.near_r), channel_id=1, source_target_pairs={{0,1},{1,0},{2,3},{3,2},{4,5},{5,4},{6,7},{7,6},{8,9},{9,8},{10,11... | collective-permute-start | bytes 1769480 | tf_op jit(solution)/shard_map/ppermute | solution.py:577

commit v11 on v10

--- a/solution.py
+++ b/solution.py
@@ -571,7 +571,7 @@
         swap = [(d, d + 1 - 2 * (d % 2)) for d in range(group)]
         near = [lax.ppermute(tail_r, "data", to_right), lax.ppermute(tail_l, "data", to_left)]
         params = store_step(functools.partial(store_params_kernel, group), params, 2 * (group // 2 + 2))
-        first = mom_new.shape[0] // 4
+        first = 3 * mom_new.shape[0] // 8
         mom_out = store_step(functools.partial(store_first_kernel, first), mom_new, first)
         *near, params, mom_out = lax.optimization_barrier((*near, params, mom_out))
         far = [lax.ppermute(piece, "data", swap) for piece in near]

time: 281 us -> 281 us (level)
  no operation moved by 1% of the time
where the time goes in v11:
time: 281 us
  Pallas kernels  276 us (98%)
  starting transfers between devices  4.06 us (1%)
    pallas_call x1, Pallas kernels, muon_step(): pl.pallas_call(functools.partial(muon_kernel, group), in_specs=[hbm, hbm,...  258 us
    pallas_call x2, Pallas kernels, store_step(): pl.pallas_call(kernel, in_specs=[pl.BlockSpec(memory_space=pltpu.VMEM)],...  13.4 us
  transfers between devices with their start and end apart: 4, of which 0 were waited for; matrix products, arithmetic and copies ran while one was open for 0% of the time, Pallas kernels for 6%

profile of v11, /device:TPU:81, one launch (start us, length us, event | category | flops | bytes accessed | tf_op | source)
XLA Modules:
  0.0 280.6 jit_solution(13086367157120418278)
XLA Ops:
  0.6 258.4 %shard_map.50 = (bf16[8,768,3072]{2,1,0:T(8,128)(2,1)S(1)}, f32[8,96,3072]{2,1,0:T(8,128)S(1)}, f32[4,96,3072]{2,1,0:T(8,128)}, bf16[96,3072]{1,0:T(8,128)(2,1)}, bf16[96,3072]{1,0:T(8,128)(2,1)}) custom-call(f32[8,96,3072]{2,1,0:T(8,128)} %mom.1, bf16[8,96,3072]{2,1,0:T(8,128)(2,1)} %grad.1, f32[8,96,3072]{2,1,0:T(8,128)} %w.1), custom_call_target="tpu_custom_call" | custom-call | tf_op jit(solution)/shard_map/pallas_call | solution.py:446
  259.0 0.3 collective-permute-start
  259.4 2.4 collective-permute-start.1
  261.8 11.5 %shard_map.51.params = bf16[8,768,3072]{2,1,0:T(8,128)(2,1)} custom-call(bf16[8,768,3072]{2,1,0:T(8,128)(2,1)S(1)} %get-tuple-element.15.src), custom_call_target="tpu_custom_call" | custom-call | flops 18874368000 | bytes 37748736 | tf_op jit(solution)/shard_map/pallas_call | solution.py:524
  273.4 1.8 shard_map.52._
  275.2 0.0 collective-permute-done.near_l
  275.2 0.0 collective-permute-done.1.near_r
  275.2 1.2 collective-permute-start.2
  276.4 0.1 collective-permute-start.3
  276.5 2.6 shard_map.53
  279.1 0.0 collective-permute-done.2.far_l
  279.1 0.0 collective-permute-done.3.far_r
  279.1 1.5 shard_map.54
Async XLA Ops:
  259.0 16.1 %collective-permute-start = (bf16[96,3072]{1,0:T(8,128)(2,1)}, bf16[96,3072]{1,0:T(8,128)(2,1)S(1)}, u32[]{:S(2)}, u32[]{:S(2)}) collective-permute-start(bf16[96,3072]{1,0:T(8,128)(2,1)} %get-tuple-element.13), channel_id=1, source_target_pairs={{0,2},{1,3},{2,4},{3,5},{4,6},{5,7},{6,0},{7,1},{8,10},{9,11},{10,... | collective-permute-start | bytes 1769480 | tf_op jit(solution)/shard_map/ppermute | solution.py:572
  259.4 15.8 %collective-permute-start.1 = (bf16[96,3072]{1,0:T(8,128)(2,1)}, bf16[96,3072]{1,0:T(8,128)(2,1)S(1)}, u32[]{:S(2)}, u32[]{:S(2)}) collective-permute-start(bf16[96,3072]{1,0:T(8,128)(2,1)} %get-tuple-element.14), channel_id=1, source_target_pairs={{0,6},{1,7},{2,0},{3,1},{4,2},{5,3},{6,4},{7,5},{8,14},{9,15},{10,... | collective-permute-start | bytes 1769480 | tf_op jit(solution)/shard_map/ppermute | solution.py:572
  275.2 3.9 %collective-permute-start.2 = (bf16[96,3072]{1,0:T(8,128)(2,1)S(1)}, bf16[96,3072]{1,0:T(8,128)(2,1)S(1)}, u32[]{:S(2)}, u32[]{:S(2)}) collective-permute-start(bf16[96,3072]{1,0:T(8,128)(2,1)S(1)} %collective-permute-done.near_l), channel_id=1, source_target_pairs={{0,1},{1,0},{2,3},{3,2},{4,5},{5,4},{6,7},{7,6},{8,9},{9,8},{10,11... | collective-permute-start | bytes 1769480 | tf_op jit(solution)/shard_map/ppermute | solution.py:577
  276.4 2.8 collective-permute-start.3
